TPU v7x, 512 devices: a whole 4x8x8 slice. The times are simulated.
512 devices in a mesh: expert: 64 (over z_lo, y, x), shard: 8 (over z_hi, core).
Axes of the slice: x: 4, y: 8, z: 8 (z_hi: 4, z_lo: 2; z = z_hi * 2 + z_lo), core: 2. Of those that a mesh axis runs over, the one named last changes fastest.
Arguments:
- w_gate: float32 [64, 2048, 1024], P('expert', 'shard'), may hold values from -0.125 to 0.125
- avg_gate: float32 [64, 2048, 1024], P('expert', 'shard'), may hold values from -0.125 to 0.125
- w_up: float32 [64, 2048, 1024], P('expert', 'shard'), may hold values from -0.125 to 0.125
- avg_up: float32 [64, 2048, 1024], P('expert', 'shard'), may hold values from -0.125 to 0.125
- mix_share: float32 [64], P('expert'), may hold values from 0.2 to 0.8
- router_weight: float32 [2048, 64], P('shard', 'expert'), may hold values from -0.125 to 0.125
- router_gain: float32 [2048], P('shard'), may hold values from 0.25 to 1.75
Outputs:
- serve_gate: bfloat16 [64, 1024, 2048], P('expert')
- serve_up: bfloat16 [64, 1024, 2048], P('expert')
- serve_router: bfloat16 [2048, 64], replicated
All inputs are finite; a program needn't handle non-finite values.
Results may differ from a plain program's by a relative error of at most 0.001.
Values may be sent and summed in bfloat16 or wider, within the bound.
A program may use at most 64 MiB of HBM per device.

v0:
```python
import jax
import jax.numpy as jnp
from jax import lax
from jax.sharding import PartitionSpec as P


def sent_together(arrays, axis, dim, along):
    ends, at = ([], 0)
    for a in arrays[:-1]:
        at += a.shape[along]
        ends.append(at)
    both = jnp.concatenate(arrays, axis=along)
    return tuple(jnp.split(lax.all_gather(both, axis, axis=dim, tiled=True), ends, axis=along))


def joined_along(parts, dim):
    parts = jnp.moveaxis(parts, 0, dim)
    lengths = parts.shape
    return parts.reshape(*lengths[:dim], lengths[dim] * lengths[dim + 1], *lengths[dim + 2 :])


def sent_to_all(x, axis):
    length = lax.axis_size(axis)
    return lax.all_to_all(jnp.broadcast_to(x[None], (length, *x.shape)), axis, 0, 0, tiled=True)


def gathered_copies(x, axis, dim):
    return joined_along(sent_to_all(x, axis), dim)


def local(w_gate, avg_gate, w_up, avg_up, mix_share, router_weight, router_gain):
    fresh_gate = mix_share[:, None, None] * w_gate + (1.0 - mix_share[:, None, None]) * avg_gate
    fresh_up = mix_share[:, None, None] * w_up + (1.0 - mix_share[:, None, None]) * avg_up
    narrow_gate, narrow_up = (fresh_gate.astype(jnp.bfloat16), fresh_up.astype(jnp.bfloat16))
    serve_gate, serve_up = sent_together((narrow_gate, narrow_up), "shard", 1, 0)
    serve_gate = jnp.transpose(serve_gate, (0, 2, 1))
    serve_up = jnp.transpose(serve_up, (0, 2, 1))
    part_router = (router_weight * router_gain[:, None]).astype(jnp.bfloat16)
    row_router = gathered_copies(part_router, "shard", 0)
    serve_router = gathered_copies(row_router, "expert", 1)
    return (serve_gate, serve_up, serve_router)


def solution(mesh):
    return jax.shard_map(
        local,
        mesh=mesh,
        in_specs=(
            P("expert", "shard", None),
            P("expert", "shard", None),
            P("expert", "shard", None),
            P("expert", "shard", None),
            P("expert"),
            P("shard", "expert"),
            P("shard"),
        ),
        out_specs=(P("expert", None, None), P("expert", None, None), P()),
        check_vma=False,
    )
```

profile of v0, /device:TPU:1, one launch (start us, length us, event | category | flops | bytes accessed | tf_op | source)
XLA Modules:
  0.0 134.6 jit_solution(16616703295714073848)
XLA Ops:
  7.2 0.0 all-gather.2.cloned.1.call-start
  7.9 1.6 %copy.22 = f32[1,256,1024]{1,2,0:T(8,128)S(1)} copy(f32[1,256,1024]{2,1,0:T(8,128)} %param.7) | data formatting | bytes 2097152 | tf_op args[0]
  9.4 1.6 %copy.23 = f32[1,256,1024]{1,2,0:T(8,128)S(1)} copy(f32[1,256,1024]{2,1,0:T(8,128)} %param.8) | data formatting | bytes 2097152 | tf_op args[1]
  11.0 1.6 %copy.24 = f32[1,256,1024]{1,2,0:T(8,128)S(1)} copy(f32[1,256,1024]{2,1,0:T(8,128)} %param.9) | data formatting | bytes 2097152 | tf_op args[2]
  12.5 2.5 %copy.25 = f32[1,256,1024]{1,2,0:T(8,128)} copy(f32[1,256,1024]{2,1,0:T(8,128)} %param.10) | data formatting | bytes 2097152 | tf_op args[3]
  15.1 0.0 copy-start
  15.1 0.0 copy-start.1
  15.1 1.6 %add_convert_fusion = (bf16[1,256,1024]{1,2,0:T(8,128)(2,1)S(1)}, bf16[1,256,1024]{1,2,0:T(8,128)(2,1)S(1)}) fusion(f32[1,256,1024]{1,2,0:T(8,128)} %copy.25, f32[1,256,1024]{1,2,0:T(8,128)S(1)} %copy.24, f32[]{:T(128)} %bitcast.1, f32[]{:T(128)} %bitcast.21, f32[1,256,1024]{1,2,0:T(8,128)S(1)} %copy.23, f32[1,256,1024]{1,2,0:T(8,128)S(1)} %copy.22), kind=kLoop, calls=%fused_computation.3 | loop fusion | flops 2097152 | bytes 5242888 | tf_op jit(solution)/shard_map/convert_element_type | solution.py:34
  16.6 1.1 pad_maximum_fusion
  17.7 0.0 all-gather.2.cloned.1.call-update
  17.7 0.0 copy-done
  17.7 0.0 copy-done.1
  17.8 0.5 broadcast.6
  18.3 0.7 reduce.4
  19.0 18.6 %all_to_all.10 = bf16[8,2,128]{2,1,0:T(2,128)(2,1)S(1)} all-to-all(bf16[8,2,128]{2,1,0:T(2,128)(2,1)S(1)} %reshape.26), channel_id=1, replica_groups=mesh['expert'=64,'shard'=8] {'shard'}, dimensions={0} | all-to-all | bytes 8192 | tf_op jit(solution)/shard_map/all_to_all | solution.py:24
  37.7 0.3 broadcast_bitcast_fusion
  37.9 2.2 %reduce.5 = bf16[64,2048]{1,0:T(8,128)(2,1)S(1)} reduce(bf16[64,1,2048]{2,1,0:T(2,128)(2,1)S(1)} %broadcast_bitcast_fusion, bf16[]{:T(256)} %broadcast.6), dimensions={1}, to_apply=%broadcast_bitcast_fusion.reduce_sub_computation | reduce | bytes 524290
  40.1 0.2 reshape.28
  40.3 26.6 %all_to_all.11 = bf16[64,2,1024]{2,1,0:T(2,128)(2,1)S(1)} all-to-all(bf16[64,2,1024]{2,1,0:T(2,128)(2,1)S(1)} %reshape.28), channel_id=1, replica_groups=mesh['expert'=64,'shard'=8] {'expert'}, dimensions={0} | all-to-all | bytes 524288 | tf_op jit(solution)/shard_map/all_to_all | solution.py:24
  66.9 0.2 reshape.29
  67.2 0.9 copy.29
  68.0 53.6 %all-gather.2.cloned.1.call-done = bf16[2,2048,1024]{1,2,0:T(8,128)(2,1)} async-done(((bf16[2,256,1024]{1,2,0:T(8,128)(2,1)}), bf16[2,2048,1024]{1,2,0:T(8,128)(2,1)}) %all-gather.2.cloned.1.call-update) | async-done | bytes 8388624 | tf_op jit(solution)/shard_map/all_gather | solution.py:13
  121.6 6.1 %slice_bitcast_fusion = (bf16[1,1024,2048]{2,1,0:T(8,128)(2,1)}, bf16[1,1024,2048]{2,1,0:T(8,128)(2,1)}) fusion(bf16[2,2048,1024]{1,2,0:T(8,128)(2,1)} %all-gather.2.cloned.1.call-done), kind=kLoop, calls=%fused_computation | loop fusion | bytes 16777216 | tf_op jit(solution)/shard_map/transpose | solution.py:37
  (6 shorter events, 0.1 us)
Async XLA Ops:
  7.2 114.5 %all-gather.2.cloned.1.call-start = ((), (), s32[]{:S(2)}) async-start(), calls=%async_computation.2 | async-start | bytes 9437184 | tf_op jit(solution)/shard_map/all_gather | solution.py:13
  15.1 2.6 %copy-start = (f32[256,1]{0,1:T(1,128)S(1)}, f32[256,1]{0,1:T(1,128)}, u32[]{:S(2)}) copy-start(f32[256,1]{0,1:T(1,128)} %param.12) | copy-start | bytes 3076
  15.1 2.7 %copy-start.1 = (f32[256]{0:T(256)S(1)}, f32[256]{0:T(256)}, u32[]{:S(2)}) copy-start(f32[256]{0:T(256)} %param.13) | copy-start | bytes 3076
Sparse Core Ops, SparseCore 0:
  17.8 103.7 all-gather.1
where the time goes:
time: 135 us
  waiting for transfers between devices  53.6 us (40%)
  blocking collectives  45.3 us (34%)
  local copies, waits for them, and re-layouts  15.5 us (11%)
  between operations  14.8 us (11%)
  other arithmetic  5.48 us (4%)
    all_gather x1, waiting for transfers between devices, sent_together(): lax.all_gather(both, axis, axis=dim, tiled=True)  53.6 us
    all_to_all x2, blocking collectives, sent_to_all(): lax.all_to_all(jnp.broadcast_to(x[None], (length, *x.shape)), axis, 0, 0,...  45.3 us
    unnamed x16, local copies, waits for them, and re-layouts  8.44 us
    transpose x1, local copies, waits for them, and re-layouts, local(): serve_up = jnp.transpose(serve_up, (0, 2, 1))  6.14 us
    unnamed x2, other arithmetic  2.84 us
  transfers between devices with their start and end apart: 1, of which 1 were waited for; matrix products, arithmetic and copies ran while one was open for 4% of the time, Pallas kernels for 0%

commit v1 on v0

v1 whole, which is shorter than its diff:
```python
import jax
import jax.numpy as jnp
from jax import lax
from jax.experimental import pallas as pl
from jax.experimental.pallas import tpu as pltpu
from jax.sharding import PartitionSpec as P

MESH = pl.DeviceIdType.MESH
D_MODEL, D_EXPERT, EXPERTS, SHARDS = 2048, 1024, 64, 8
WIDE = D_MODEL // SHARDS
ROWS = 128
CHUNKS = D_EXPERT // ROWS
X, Y, Z = 4, 8, 8
EARLY = 4
PARTS = 4


def kernel(wg, ag, wu, au, rw_any, gain_any, mix, gate, up, router, held, held_sem, rw, gain, small_sem, ring, flat,
           ici_send, ici_recv, core_send, core_recv, r_send, r_recv):
    e, s = lax.axis_index("expert"), lax.axis_index("shard")
    z_lo, y, x = e // (Y * X), (e // X) % Y, e % X
    z_hi, c = s // 2, s % 2
    z = 2 * z_hi + z_lo

    def at(x_, y_, z_, c_):
        return {"expert": (z_ % 2) * (Y * X) + y_ * X + x_, "shard": (z_ // 2) * 2 + c_}

    fore, back = at(x, y, (z + 2) % Z, c), at(x, y, (z + Z - 2) % Z, c)
    mate = at(x, y, z, 1 - c)
    steps = {
        "z": (at(x, y, (z + 1) % Z, c), at(x, y, (z + Z - 1) % Z, c)),
        "x": (at((x + 1) % X, y, z, c), at((x + X - 1) % X, y, z, c)),
        "y": (at(x, (y + 1) % Y, z, c), at(x, (y + Y - 1) % Y, z, c)),
    }

    def loads(j):
        cols = pl.ds(pl.multiple_of(j * ROWS, ROWS), ROWS)
        return [pltpu.make_async_copy(ref.at[0, :, cols], held.at[i, :, cols], held_sem.at[i, j])
                for i, ref in enumerate((wg, ag, wu, au))]

    small = [pltpu.make_async_copy(a, b, small_sem.at[i])
             for i, (a, b) in enumerate(((rw_any, rw), (gain_any, gain)))]
    for j in range(CHUNKS):
        for copy in loads(j):
            copy.start()
    small[0].start()
    small[1].start()

    barrier = pltpu.get_barrier_semaphore()
    peers = [fore, back, mate, *steps["z"], *steps["x"], *steps["y"]]
    for peer in peers:
        pl.semaphore_signal(barrier, inc=1, device_id=peer, device_id_type=MESH)

    share = mix[...]
    rest = 1.0 - share

    def columns(shard):
        return pl.ds(pl.multiple_of(shard * WIDE, WIDE), WIDE)

    def compute(j):
        cols = pl.ds(pl.multiple_of(j * ROWS, ROWS), ROWS)
        for copy in loads(j):
            copy.wait()
        for k, out in enumerate((gate, up)):
            fresh = share * held[2 * k, :, cols] + rest * held[2 * k + 1, :, cols]
            out[cols, columns(s)] = fresh.T.astype(jnp.bfloat16)

    def block(out, shard, j):
        return out.at[pl.ds(pl.multiple_of(j * ROWS, ROWS), ROWS), columns(shard)]

    def copy(out, shard, j, to, send, recv):
        ref = block(out, shard, j)
        return pltpu.make_async_remote_copy(ref, ref, send, recv, device_id=to, device_id_type=MESH)

    def hop(lane, kind, j, shard):
        out = (gate, up)[(kind + lane) % 2] if kind < 2 else (gate, up)[lane]
        return copy(out, shard, j, (fore, back)[lane], ici_send.at[lane, kind, j], ici_recv.at[lane, kind, j])

    def across(lane, kind, j, shard):
        if lane == 2:
            out = (gate, up)[kind]
        else:
            out = (gate, up)[(kind + lane) % 2] if kind < 2 else (gate, up)[lane]
        return copy(out, shard, j, mate, core_send.at[lane, kind, j], core_recv.at[lane, kind, j])

    def from_(lane, kind, z_step=0):
        far = 2 if kind == 2 else 1
        d = (4 - far if lane == 0 else far)
        return 2 * ((z_hi + d) % 4)

    def post(i, ref, to):
        return pltpu.make_async_remote_copy(
            ref, ref, r_send.at[i], r_recv.at[i], device_id=to, device_id_type=MESH)

    def piece(k):
        return ring.at[c, y, x, (z + k + Z) % Z]

    def row(k):
        return ring.at[c, y, (x + k + X) % X]

    def plane(k):
        return ring.at[c, (y + k + Y) % Y]

    zp, zm = steps["z"]
    xp, xm = steps["x"]
    yp, ym = steps["y"]
    posts = [
        (piece(0), zp, piece(-1)), (piece(0), zm, piece(1)), (piece(0), fore, piece(-2)), (piece(0), back, piece(2)),
        (piece(-2), zp, piece(-3)), (piece(2), zm, piece(3)), (piece(-2), fore, piece(-4)),
        (row(0), xp, row(-1)), (row(0), xm, row(1)), (row(-1), xp, row(-2)),
        (plane(0), yp, plane(-1)), (plane(0), ym, plane(1)), (plane(-1), yp, plane(-2)), (plane(1), ym, plane(2)),
        (plane(-2), yp, plane(-3)), (plane(2), ym, plane(3)), (plane(-3), yp, plane(-4)),
        (ring.at[c], mate, ring.at[1 - c]),
    ]
    rounds = [
        ((), (0, 1, 2, 3)), ((2, 3), (4, 5, 6)), ((0, 1, 4, 5, 6), (7, 8)), ((7,), (9,)), ((8, 9), (10, 11)),
        ((10, 11), (12, 13)), ((12, 13), (14, 15)), ((14,), (16,)), ((15, 16), (17,)), ((17,), ()),
    ]

    def turn(n):
        waits, sends = rounds[n]
        for i in waits:
            post(i, posts[i][2], posts[i][1]).wait_recv()
        for i in sends:
            post(i, posts[i][0], posts[i][1]).start()

    compute(0)
    small[0].wait()
    small[1].wait()
    ring[c, y, x, z] = rw[...] * gain[...]
    compute(1)
    pl.semaphore_wait(barrier, len(peers))
    turn(0)

    def begin(j):
        for lane in range(2):
            hop(lane, 0, j, s).start()
            across(2, lane, j, s).start()

    begin(0)
    for j in range(2, CHUNKS):
        compute(j)
        begin(j - 1)
        if j == EARLY:
            turn(1)
    begin(CHUNKS - 1)

    def second(j, _):
        for lane in range(2):
            hop(lane, 1, j, s).start()
        return 0

    lax.fori_loop(0, CHUNKS, second, 0)

    for j in range(CHUNKS):
        for lane in range(2):
            shard = from_(lane, 0) + c
            hop(lane, 0, j, shard).wait_recv()
            hop(lane, 2, j, shard).start()
            across(lane, 0, j, shard).start()
        if j + 2 < len(rounds):
            turn(j + 2)

    def lay(i, _):
        yy, xx = i // X, i % X
        for zz in range(Z):
            for cc in range(2):
                lo = (2 * (zz // 2) + cc) * WIDE
                flat[pl.ds((zz % 2) * (Y * X) + i, 1), lo : lo + WIDE] = ring[cc, yy, xx, zz]
        return 0

    lax.fori_loop(0, Y * X, lay, 0)
    router[...] = flat[...].astype(jnp.bfloat16)

    for kind in (1, 2):
        def across_only(j, _):
            for lane in range(2):
                shard = from_(lane, kind) + c
                hop(lane, kind, j, shard).wait_recv()
                across(lane, kind, j, shard).start()
            return 0

        lax.fori_loop(0, CHUNKS, across_only, 0)

    def finish(j, _):
        for lane in range(2):
            for kind in range(3):
                hop(lane, kind, j, s).wait_send()
                across(lane, kind, j, s).wait_send()
                across(lane, kind, j, from_(lane, kind) + 1 - c).wait_recv()
        for kind in range(2):
            across(2, kind, j, s).wait_send()
            across(2, kind, j, 2 * z_hi + 1 - c).wait_recv()
        return 0

    lax.fori_loop(0, CHUNKS, finish, 0)
    for i, (sent, to, _) in enumerate(posts):
        post(i, sent, to).wait_send()


def store(gate, up, router, gate_out, up_out, router_out, sem):
    copies = []
    for k, (a, b) in enumerate(((gate, gate_out), (up, up_out))):
        for i in range(PARTS):
            rows = pl.ds(i * (D_EXPERT // PARTS), D_EXPERT // PARTS)
            copies.append(pltpu.make_async_copy(a.at[rows], b.at[rows], sem.at[k, i]))
    copies.append(pltpu.make_async_copy(router, router_out, sem.at[2, 0]))
    for copy in copies:
        copy.start()
    for copy in copies:
        copy.wait()


def local(w_gate, avg_gate, w_up, avg_up, mix_share, router_weight, router_gain):
    out = jax.ShapeDtypeStruct((D_EXPERT, D_MODEL), jnp.bfloat16)
    hbm = pl.BlockSpec(memory_space=pltpu.HBM)
    vmem = pl.BlockSpec(memory_space=pltpu.VMEM)
    dma = pltpu.SemaphoreType.DMA
    gate, up, router = pl.pallas_call(
        kernel,
        out_shape=(out, out, jax.ShapeDtypeStruct((EXPERTS, D_MODEL), jnp.bfloat16)),
        in_specs=[hbm] * 6 + [vmem],
        out_specs=(vmem, vmem, vmem),
        scratch_shapes=[
            pltpu.VMEM((4, WIDE, D_EXPERT), jnp.float32),
            dma((4, CHUNKS)),
            pltpu.VMEM((1, WIDE), jnp.float32),
            pltpu.VMEM((1, WIDE), jnp.float32),
            dma((2,)),
            pltpu.VMEM((2, Y, X, Z, 1, WIDE), jnp.float32),
            pltpu.VMEM((EXPERTS, D_MODEL), jnp.float32),
            dma((2, 3, CHUNKS)),
            dma((2, 3, CHUNKS)),
            dma((3, 3, CHUNKS)),
            dma((3, 3, CHUNKS)),
            dma((18,)),
            dma((18,)),
        ],
        compiler_params=pltpu.CompilerParams(
            collective_id=0, has_side_effects=True, vmem_limit_bytes=40 * 2**20),
        name="mix_and_gather",
    )(*(pltpu.with_memory_space_constraint(a, pltpu.HBM) for a in (
        w_gate, avg_gate, w_up, avg_up, router_weight.reshape(1, WIDE), router_gain.reshape(1, WIDE))),
        mix_share.reshape(1, 1))
    gate, up, router = pl.pallas_call(
        store,
        out_shape=(out, out, jax.ShapeDtypeStruct((EXPERTS, D_MODEL), jnp.bfloat16)),
        in_specs=[vmem] * 3,
        out_specs=(hbm,) * 3,
        scratch_shapes=[dma((3, PARTS))],
        compiler_params=pltpu.CompilerParams(vmem_limit_bytes=2**20),
        name="store",
    )(gate, up, router)
    return gate[None], up[None], router.T


def solution(mesh):
    return jax.shard_map(
        local,
        mesh=mesh,
        in_specs=(
            P("expert", "shard", None),
            P("expert", "shard", None),
            P("expert", "shard", None),
            P("expert", "shard", None),
            P("expert"),
            P("shard", "expert"),
            P("shard"),
        ),
        out_specs=(P("expert", None, None), P("expert", None, None), P()),
        check_vma=False,
    )
```

time: 135 us -> 91.4 us (0.68)
  Pallas kernels: 0 us -> 89.9 us
  waiting for transfers between devices: 53.6 us -> 0 us
  blocking collectives: 45.3 us -> 0 us
  local copies, waits for them, and re-layouts: 15.5 us -> 0 us
  between operations: 14.8 us -> 1.29 us
  other arithmetic: 5.48 us -> 0 us
    pallas_call x0 -> x2, Pallas kernels: none -> 89.9 us  [the longest x1 86.5 us: local(): pl.pallas_call(kernel, out_shape=(out, out, jax.ShapeDtypeStruct((EXPERTS...]
    all_gather x1 -> x0, waiting for transfers between devices: 53.6 us -> none  [sent_together(): lax.all_gather(both, axis, axis=dim, tiled=True)]
    all_to_all x2 -> x0, blocking collectives: 45.3 us -> none  [sent_to_all(): lax.all_to_all(jnp.broadcast_to(x[None], (length, *x.shape)), axis, 0, 0,...]
    unnamed x16 -> x0, local copies, waits for them, and re-layouts: 8.44 us -> none
    transpose x1 -> x0, local copies, waits for them, and re-layouts: 6.14 us -> none  [local(): serve_up = jnp.transpose(serve_up, (0, 2, 1))]
    unnamed x2 -> x0, other arithmetic: 2.84 us -> none
    convert_element_type x2 -> x0, other arithmetic: 1.57 us -> none  [the longest x1 1.55 us: local(): fresh_up.astype(jnp.bfloat16)]
  transfers between devices with their start and end apart: 1 -> 0, of which waited for: 1 -> 0; matrix products, arithmetic and copies ran while one was open for 4% -> 0% of each run, Pallas kernels for 0% -> 0%
where the time goes in v1:
time: 91.4 us; the launch traced here: 91.2 us
  Pallas kernels  89.9 us (98%)
  between operations  1.29 us (1%)
    pallas_call x1, Pallas kernels, local(): pl.pallas_call(kernel, out_shape=(out, out, jax.ShapeDtypeStruct((EXPERTS...  86.5 us
    pallas_call x1, Pallas kernels, local(): pl.pallas_call(store, out_shape=(out, out, jax.ShapeDtypeStruct((EXPERTS,...  3.45 us

profile of v1, /device:TPU:1, one launch (start us, length us, event | category | flops | bytes accessed | tf_op | source)
XLA Modules:
  0.0 91.2 jit_solution(12984875756497173225)
XLA Ops:
  1.3 86.5 %mix_and_gather.1 = (bf16[1024,2048]{1,0:T(8,128)(2,1)S(1)}, bf16[1024,2048]{1,0:T(8,128)(2,1)S(1)}, bf16[64,2048]{1,0:T(8,128)(2,1)S(1)}) custom-call(f32[1,256,1024]{2,1,0:T(8,128)} %wg.1, f32[1,256,1024]{2,1,0:T(8,128)} %ag.1, f32[1,256,1024]{2,1,0:T(8,128)} %wu.1, f32[1,256,1024]{2,1,0:T(8,128)} %au.1, f32[1,256]{1,0:T(1,128)} %bitcast.7, ...), custom_call_target="tpu_custom_call" | custom-call | tf_op jit(solution)/shard_map/mix_and_gather/pallas_call | solution.py:219
  87.8 3.5 %store.1 = (bf16[1024,2048]{1,0:T(8,128)(2,1)}, bf16[1024,2048]{1,0:T(8,128)(2,1)}, bf16[64,2048]{1,0:T(8,128)(2,1)}) custom-call(bf16[1024,2048]{1,0:T(8,128)(2,1)S(1)} %get-tuple-element.9.gate, bf16[1024,2048]{1,0:T(8,128)(2,1)S(1)} %get-tuple-element.10.up, bf16[64,2048]{1,0:T(8,128)(2,1)S(1)} %get-tuple-element.11.router), custom_call_target="tpu_custom_call" | custom-call | tf_op jit(solution)/shard_map/store/pallas_call | solution.py:245

commit v2 on v0

v2 whole, which is shorter than its diff:
```python
import jax
import jax.numpy as jnp
from jax import lax
from jax.experimental import pallas as pl
from jax.experimental.pallas import tpu as pltpu
from jax.sharding import PartitionSpec as P

MESH = pl.DeviceIdType.MESH
D_MODEL, D_EXPERT, EXPERTS, SHARDS = 2048, 1024, 64, 8
WIDE = D_MODEL // SHARDS
ROWS = 128
CHUNKS = D_EXPERT // ROWS
X, Y, Z = 4, 8, 8
FORE, BACK, MATE, ZP, ZM, XP, XM, YP, YM = range(9)
OPPOSITE = (BACK, FORE, MATE, ZM, ZP, XM, XP, YM, YP)
GROUPS = ((0, 1), (1, 3), (4, 4))
OTHER = ((0, 4), (4, 4))
PASSED = ((0, 1), (1, 3), (4, 2), (6, 1), (7, 1))
SHIFT = 0
PARTS = 4


def kernel(wg, ag, wu, au, rw_any, gain_any, mix, gate, up, router, held, load_sem, small, small_sem, ring, flat,
           ready, first_recv, second_recv, passed_recv, ici_send, core_sem, r_send, r_recv):
    e, s = lax.axis_index("expert"), lax.axis_index("shard")
    x, y, z_lo = e & (X - 1), (e >> 2) & (Y - 1), e >> 5
    z_hi, c = s >> 1, s & 1
    z = 2 * z_hi + z_lo

    def columns_of(g):
        return pl.ds(GROUPS[g][0] * ROWS, GROUPS[g][1] * ROWS)

    for i, ref in enumerate((rw_any, gain_any)):
        pltpu.make_async_copy(ref, small.at[i], small_sem).start()
    for g in range(len(GROUPS)):
        for k in (1, 0):
            for i, ref in enumerate(((wg, ag), (wu, au))[k]):
                pltpu.make_async_copy(ref.at[0, :, columns_of(g)], held.at[2 * k + i, :, columns_of(g)], load_sem.at[k, g]).start()

    def loaded(k, g):
        ref = held.at[2 * k : 2 * k + 2, :, columns_of(g)]
        pltpu.make_async_copy(ref, ref, load_sem.at[k, g]).wait()

    def place(dx=0, dy=0, dz=0, dc=0):
        return (x + dx) & (X - 1), (y + dy) & (Y - 1), (z + dz) & (Z - 1), (c + dc) & 1

    def device(p):
        return {"expert": ((p[2] & 1) << 5) + (p[1] << 2) + p[0], "shard": (p[2] & 6) + p[3]}

    def rank(p):
        order = (p[2] << 6) + (p[1] << 3) + (p[0] << 1) + 1 - p[3]
        return jnp.where(order == 1, 2 * X * Y * Z, order)

    places = [place(dz=2), place(dz=-2), place(dc=1), place(dz=1), place(dz=-1), place(dx=1), place(dx=-1), place(dy=1), place(dy=-1)]
    near = [device(p) for p in places]
    own_rank = rank(place())
    earlier = [rank(p) < own_rank for p in places]
    lanes = (FORE, BACK)

    barrier = pltpu.get_barrier_semaphore()
    for k in range(9):
        @pl.when(jnp.logical_not(earlier[k]))
        def _():
            pl.semaphore_signal(barrier, inc=1, device_id=near[k], device_id_type=MESH)
    def answer():
        before = sum(a.astype(jnp.int32) for a in earlier)

        @pl.when(before > 0)
        def _():
            pl.semaphore_wait(barrier, before)

        for k in range(9):
            @pl.when(earlier[k])
            def _():
                pl.semaphore_signal(ready.at[min(OPPOSITE[k], ZP)], inc=1, device_id=near[k], device_id_type=MESH)

    def allow(k):
        @pl.when(jnp.logical_not(earlier[k]))
        def _():
            pl.semaphore_wait(ready.at[k], 1)

    def allow_rest():
        after = sum(1 - earlier[k].astype(jnp.int32) for k in range(ZP, 9))

        @pl.when(after > 0)
        def _():
            pl.semaphore_wait(ready.at[ZP], after)

    share = mix[...]
    rest = 1.0 - share

    def columns(shard):
        return pl.ds(pl.multiple_of(shard * WIDE, WIDE), WIDE)

    def rows(j, n=1):
        return pl.ds(pl.multiple_of(j * ROWS, ROWS), n * ROWS)

    def compute(k, j):
        fresh = share * held[2 * k, :, rows(j)] + rest * held[2 * k + 1, :, rows(j)]
        (gate, up)[k][rows(j), columns(s)] = fresh.T.astype(jnp.bfloat16)

    def copy(k, shard, j, n, to, send, recv):
        ref = (gate, up)[k].at[rows(j, n), columns(shard)]
        return pltpu.make_async_remote_copy(ref, ref, send, recv, device_id=near[to], device_id_type=MESH)

    def first(lane, i, shard):
        return copy(lane, shard, *GROUPS[i], lanes[lane], ici_send.at[lane], first_recv.at[lane, i])

    def second(lane, i, shard):
        return copy(1 - lane, shard, *OTHER[i], lanes[lane], ici_send.at[lane], second_recv.at[i])

    def passed(lane, i, shard, send=2):
        return copy(lane, shard, *PASSED[i], lanes[lane], ici_send.at[send], passed_recv.at[lane, i])

    def across(k, shard, j, n=1):
        return copy(k, shard, j, n, MATE, core_sem.at[0], core_sem.at[1])

    def arriving(lane, far):
        return ((z_hi + (4 - far if lane == 0 else far)) & 3) * 2 + c

    def sent(ref, sem):
        pltpu.make_async_remote_copy(ref, ref, sem, core_sem.at[1], device_id=near[MATE], device_id_type=MESH).wait_send()

    def post(ref, to, i):
        return pltpu.make_async_remote_copy(
            ref, ref, r_send.at[(0, 0, 1, 1, 2, 2, 2, 2, 3)[i]], r_recv.at[i], device_id=near[to], device_id_type=MESH)

    def piece(k):
        return ring.at[c, y, x, (z + k) & (Z - 1)]

    def row(k):
        return ring.at[c, y, (x + k) & (X - 1)]

    def plane(k):
        return ring.at[c, (y + k) & (Y - 1)]

    def landed(ref, i):
        post(ref, MATE, i).wait_recv()

    even = (z & 1) == 0
    zeroth = jnp.logical_or(z < 2, z >= 6)

    def in_turn(order, do):
        for lane in range(2):
            @pl.when(zeroth if lane == order else jnp.logical_not(zeroth))
            def _():
                do(lane)

    def admit(lane):
        allow(lanes[lane])
        post(piece(0), lanes[lane], 0).start()

    def begin(order, *which):
        in_turn(order, lambda lane: [first(lane, i, s).start() for i in which])

    with jax.named_scope("first_chunk"):
        loaded(1, 0)
        compute(1, 0)
        loaded(0, 0)
        compute(0, 0)
        pltpu.make_async_copy(small, small, small_sem).wait()
        ring[c, y, x, z] = small[0] * small[1]
    with jax.named_scope("admit_first"):
        answer()
        in_turn(0, admit)
    with jax.named_scope("compute"):
        def more(j, _):
            for k in (1, 0):
                compute(k, j)
            return 0

        for g in range(1, len(GROUPS)):
            for k in (1, 0):
                loaded(k, g)
            lax.fori_loop(GROUPS[g][0], GROUPS[g][0] + 1, more, 0)

            @pl.when(even)
            def _():
                begin(0, g - 1)

            lax.fori_loop(GROUPS[g][0] + 1, sum(GROUPS[g]), more, 0)
    with jax.named_scope("admit_second"):
        in_turn(1, admit)

        @pl.when(even)
        def _():
            begin(0, 2)
            begin(1, 0, 1)
    with jax.named_scope("z_steps"):
        allow_rest()
        post(piece(0), ZP, 1).start()
        post(piece(0), ZM, 1).start()
        landed(ring.at[c, y, x, 0:2], 0)
        post(piece(-2), ZP, 1).start()
        post(piece(2), ZM, 1).start()
        post(piece(-2), FORE, 1).start()
    with jax.named_scope("own"):
        @pl.when(even)
        def _():
            begin(1, 2)

        @pl.when(jnp.logical_not(even))
        def _():
            begin(0, 0, 1, 2)
            begin(1, 0, 1, 2)

        for i in range(len(OTHER)):
            for lane in range(2):
                second(lane, i, s).start()
    with jax.named_scope("mate_own"):
        allow(MATE)
        for k in range(2):
            across(k, s, 0, CHUNKS).start()

    def own_arrived(i):
        with jax.named_scope(f"half_a{i}"):
            for lane in range(2):
                shard = arriving(lane, 1)
                first(lane, i, shard).wait_recv()
                for p, (lo, n) in enumerate(PASSED):
                    if GROUPS[i][0] <= lo < sum(GROUPS[i]):
                        if lane == 0 and p < SHIFT:
                            @pl.when(z < 6)
                            def _():
                                passed(0, p, shard, 3).start()
                        else:
                            passed(lane, p, shard).start()
                across(lane, shard, *GROUPS[i]).start()

    def other_arrived(i):
        with jax.named_scope(f"half_b{i}"):
            copy(0, s, 0, 2 * OTHER[i][1], MATE, core_sem.at[0], second_recv.at[i]).wait_recv()
            if i < SHIFT:
                @pl.when(jnp.logical_and(z >= 2, z < 4))
                def _():
                    copy(0, arriving(1, 1), *PASSED[0], BACK, ici_send.at[4], passed_recv.at[0, 0]).start()
            for lane in range(2):
                across(1 - lane, arriving(lane, 1), *OTHER[i]).start()

    def router_rest():
        with jax.named_scope("router_x1"):
            landed(ring.at[c, y, x, 0:5], 1)
            post(row(0), XP, 2).start()
            post(row(0), XM, 2).start()
        with jax.named_scope("router_x2"):
            landed(ring.at[c, y, 0:2], 2)
            post(row(-1), XP, 3).start()
        with jax.named_scope("router_y1"):
            landed(ring.at[c, y, 0], 3)
            post(plane(0), YP, 4).start()
            post(plane(0), YM, 4).start()
        for i in range(3):
            with jax.named_scope(f"router_y{i + 2}"):
                landed(ring.at[c, 0:2], 4 + i)
                post(plane(-1 - i), YP, 5 + i).start()
                if i < 2:
                    post(plane(1 + i), YM, 5 + i).start()
        with jax.named_scope("router_mate"):
            landed(ring.at[c, 0], 7)
            post(ring.at[c], MATE, 8).start()

    def arrivals():
        own_arrived(0)
        own_arrived(1)
        other_arrived(0)
        own_arrived(2)
        other_arrived(1)

    @pl.when(even)
    def _():
        arrivals()
        router_rest()

    @pl.when(jnp.logical_not(even))
    def _():
        router_rest()
        arrivals()

    with jax.named_scope("router_end"):
        landed(ring.at[1 - c], 8)

        def lay(i, _):
            yy, xx = i >> 2, i & (X - 1)
            for zz in range(Z):
                for cc in range(2):
                    lo = (2 * (zz // 2) + cc) * WIDE
                    flat[pl.ds((zz % 2) * (Y * X) + i, 1), lo : lo + WIDE] = ring[cc, yy, xx, zz]
            return 0

        lax.fori_loop(0, Y * X, lay, 0)
        router[...] = flat[...].astype(jnp.bfloat16)
    order = [(lane, p) for p in range(len(PASSED)) for lane in range(2)]
    order = order[SHIFT:] + order[:SHIFT]
    for lane, p in order:
        with jax.named_scope(f"passed{p}_{lane}"):
            shard = arriving(lane, 2)
            passed(lane, p, shard).wait_recv()
            across(lane, shard, *PASSED[p]).start()

    with jax.named_scope("finish"):
        sent(gate.at[:, 0 : 2 * WIDE], ici_send.at[0])
        sent(gate.at[:, 0 : 2 * WIDE], ici_send.at[1])
        if SHIFT:
            n = PASSED[0][1] * ROWS
            sent(gate.at[0 : D_EXPERT - n // 2, 0 : 2 * WIDE], ici_send.at[2])
            for i, when in ((3, z < 6), (4, jnp.logical_and(z >= 2, z < 4))):
                @pl.when(when)
                def _():
                    sent(gate.at[0:n, 0:WIDE], ici_send.at[i])
        else:
            sent(gate.at[:, 0 : 2 * WIDE], ici_send.at[2])
        sent(ring.at[c, y, x, 0:7], r_send.at[0])
        sent(ring.at[c, y, 0:3], r_send.at[1])
        sent(ring.at[c, 0:7], r_send.at[2])
        sent(ring.at[c], r_send.at[3])
        sent(gate, core_sem.at[0])
        pltpu.make_async_remote_copy(gate, gate, core_sem.at[0], core_sem.at[1], device_id=near[MATE], device_id_type=MESH).wait_recv()


def store(gate, up, router, gate_out, up_out, router_out, sem):
    copies = []
    for k, (a, b) in enumerate(((gate, gate_out), (up, up_out))):
        for i in range(PARTS):
            rows = pl.ds(i * (D_EXPERT // PARTS), D_EXPERT // PARTS)
            copies.append(pltpu.make_async_copy(a.at[rows], b.at[rows], sem.at[k, i]))
    copies.append(pltpu.make_async_copy(router, router_out, sem.at[2, 0]))
    for copy in copies:
        copy.start()
    for copy in copies:
        copy.wait()


def local(w_gate, avg_gate, w_up, avg_up, mix_share, router_weight, router_gain):
    out = jax.ShapeDtypeStruct((D_EXPERT, D_MODEL), jnp.bfloat16)
    outs = (out, out, jax.ShapeDtypeStruct((EXPERTS, D_MODEL), jnp.bfloat16))
    hbm = pl.BlockSpec(memory_space=pltpu.HBM)
    vmem = pl.BlockSpec(memory_space=pltpu.VMEM)
    dma = pltpu.SemaphoreType.DMA
    gathered = pl.pallas_call(
        kernel,
        out_shape=outs,
        in_specs=[hbm] * 6 + [vmem],
        out_specs=(vmem,) * 3,
        scratch_shapes=[
            pltpu.VMEM((4, WIDE, D_EXPERT), jnp.float32),
            dma((2, len(GROUPS))),
            pltpu.VMEM((2, 1, WIDE), jnp.float32),
            dma,
            pltpu.VMEM((2, Y, X, Z, 1, WIDE), jnp.float32),
            pltpu.VMEM((EXPERTS, D_MODEL), jnp.float32),
            pltpu.SemaphoreType.REGULAR((4,)),
            dma((2, len(GROUPS))),
            dma((len(OTHER),)),
            dma((2, len(PASSED))),
            dma((5,)),
            dma((2,)),
            dma((4,)),
            dma((9,)),
        ],
        compiler_params=pltpu.CompilerParams(
            collective_id=0, has_side_effects=True, vmem_limit_bytes=40 * 2**20),
        name="mix_and_gather",
    )(*(pltpu.with_memory_space_constraint(a, pltpu.HBM) for a in (
        w_gate, avg_gate, w_up, avg_up, router_weight.reshape(1, WIDE), router_gain.reshape(1, WIDE))),
      mix_share.reshape(1, 1))
    gate, up, router = pl.pallas_call(
        store,
        out_shape=outs,
        in_specs=[vmem] * 3,
        out_specs=(hbm,) * 3,
        scratch_shapes=[dma((3, PARTS))],
        compiler_params=pltpu.CompilerParams(vmem_limit_bytes=2**20),
        name="store",
    )(*gathered)
    return gate[None], up[None], router.T


def solution(mesh):
    return jax.shard_map(
        local,
        mesh=mesh,
        in_specs=(
            P("expert", "shard", None),
            P("expert", "shard", None),
            P("expert", "shard", None),
            P("expert", "shard", None),
            P("expert"),
            P("shard", "expert"),
            P("shard"),
        ),
        out_specs=(P("expert", None, None), P("expert", None, None), P()),
        check_vma=False,
    )
```

time: 135 us -> 85.9 us (0.64)
  the two profiles are of different devices: /device:TPU:1 before, /device:TPU:127 now
where the time goes in v2:
time: 85.9 us; the launch traced here: 85.8 us
  Pallas kernels  84.5 us (98%)
  between operations  1.29 us (2%)
    pallas_call x1, Pallas kernels, local(): pl.pallas_call(kernel, out_shape=outs, in_specs=[hbm] * 6 + [vmem], out_s...  81 us
    pallas_call x1, Pallas kernels, local(): pl.pallas_call(store, out_shape=outs, in_specs=[vmem] * 3, out_specs=(hbm...  3.45 us

profile of v2, /device:TPU:127, one launch (start us, length us, event | category | flops | bytes accessed | tf_op | source)
XLA Modules:
  0.0 85.8 jit_solution(5809066089876249708)
XLA Ops:
  1.3 81.0 %mix_and_gather.1 = (bf16[1024,2048]{1,0:T(8,128)(2,1)S(1)}, bf16[1024,2048]{1,0:T(8,128)(2,1)S(1)}, bf16[64,2048]{1,0:T(8,128)(2,1)S(1)}) custom-call(f32[1,256,1024]{2,1,0:T(8,128)} %wg.1, f32[1,256,1024]{2,1,0:T(8,128)} %ag.1, f32[1,256,1024]{2,1,0:T(8,128)} %wu.1, f32[1,256,1024]{2,1,0:T(8,128)} %au.1, f32[1,256]{1,0:T(1,128)} %bitcast.7, ...), custom_call_target="tpu_custom_call" | custom-call | tf_op jit(solution)/shard_map/mix_and_gather/pallas_call | solution.py:339
  82.3 3.5 %store.1 = (bf16[1024,2048]{1,0:T(8,128)(2,1)}, bf16[1024,2048]{1,0:T(8,128)(2,1)}, bf16[64,2048]{1,0:T(8,128)(2,1)}) custom-call(bf16[1024,2048]{1,0:T(8,128)(2,1)S(1)} %get-tuple-element.9.gate, bf16[1024,2048]{1,0:T(8,128)(2,1)S(1)} %get-tuple-element.10.up, bf16[64,2048]{1,0:T(8,128)(2,1)S(1)} %get-tuple-element.11.router), custom_call_target="tpu_custom_call" | custom-call | tf_op jit(solution)/shard_map/store/pallas_call | solution.py:366

commit v3 on v2

--- a/solution.py
+++ b/solution.py
@@ -14,9 +14,11 @@
 FORE, BACK, MATE, ZP, ZM, XP, XM, YP, YM = range(9)
 OPPOSITE = (BACK, FORE, MATE, ZM, ZP, XM, XP, YM, YP)
 GROUPS = ((0, 1), (1, 3), (4, 4))
-OTHER = ((0, 4), (4, 4))
-PASSED = ((0, 1), (1, 3), (4, 2), (6, 1), (7, 1))
-SHIFT = 0
+OTHER = ((0, 2), (2, 6))
+PASSED = ((0, 1), (1, 1), (2, 2), (4, 2), (6, 1), (7, 1))
+LEFT = (0, 0, 0, 0, 0, 0, 2, 0), (2, 0, 0, 0, 1, 0, 0, 0)
+MOST = 2
+LATE = 6
 PARTS = 4
 
 
@@ -48,8 +50,8 @@
         return {"expert": ((p[2] & 1) << 5) + (p[1] << 2) + p[0], "shard": (p[2] & 6) + p[3]}
 
     def rank(p):
-        order = (p[2] << 6) + (p[1] << 3) + (p[0] << 1) + 1 - p[3]
-        return jnp.where(order == 1, 2 * X * Y * Z, order)
+        order = (p[2] << 7) + (p[1] << 4) + (p[0] << 2) + 2 - 2 * p[3]
+        return jnp.where(order == 2, (LATE << 7) - 1, order)
 
     places = [place(dz=2), place(dz=-2), place(dc=1), place(dz=1), place(dz=-1), place(dx=1), place(dx=-1), place(dy=1), place(dy=-1)]
     near = [device(p) for p in places]
@@ -146,46 +148,78 @@
             def _():
                 do(lane)
 
-    def admit(lane):
-        allow(lanes[lane])
+    def own_piece(lane):
         post(piece(0), lanes[lane], 0).start()
 
     def begin(order, *which):
         in_turn(order, lambda lane: [first(lane, i, s).start() for i in which])
 
+    def begin_other(order, *which):
+        in_turn(order, lambda lane: [second(lane, i, s).start() for i in which])
+
+    both = jnp.logical_and(even, z >= 6)
+    one = jnp.logical_and(even, z < 6)
+
     with jax.named_scope("first_chunk"):
+        answer()
         loaded(1, 0)
         compute(1, 0)
         loaded(0, 0)
         compute(0, 0)
-        pltpu.make_async_copy(small, small, small_sem).wait()
-        ring[c, y, x, z] = small[0] * small[1]
     with jax.named_scope("admit_first"):
-        answer()
-        in_turn(0, admit)
+        in_turn(0, lambda lane: allow(lanes[lane]))
+
+        @pl.when(even)
+        def _():
+            begin(0, 0)
+
+        @pl.when(both)
+        def _():
+            begin(1, 0)
     with jax.named_scope("compute"):
         def more(j, _):
             for k in (1, 0):
                 compute(k, j)
             return 0
 
-        for g in range(1, len(GROUPS)):
+        def more_of(g):
             for k in (1, 0):
                 loaded(k, g)
-            lax.fori_loop(GROUPS[g][0], GROUPS[g][0] + 1, more, 0)
-
-            @pl.when(even)
-            def _():
-                begin(0, g - 1)
-
-            lax.fori_loop(GROUPS[g][0] + 1, sum(GROUPS[g]), more, 0)
+            lax.fori_loop(GROUPS[g][0], sum(GROUPS[g]), more, 0)
+
+        more_of(1)
+        pltpu.make_async_copy(small, small, small_sem).wait()
+        ring[c, y, x, z] = small[0] * small[1]
+        in_turn(0, own_piece)
+
+        @pl.when(even)
+        def _():
+            begin(0, 1)
+
+        @pl.when(both)
+        def _():
+            in_turn(1, own_piece)
+            begin(1, 1)
+
+        @pl.when(even)
+        def _():
+            begin_other(0, 0)
+
+        more_of(2)
     with jax.named_scope("admit_second"):
-        in_turn(1, admit)
+        in_turn(1, lambda lane: allow(lanes[lane]))
+
+        @pl.when(jnp.logical_not(both))
+        def _():
+            in_turn(1, own_piece)
+
+        @pl.when(one)
+        def _():
+            begin(1, 0, 1)
 
         @pl.when(even)
         def _():
-            begin(0, 2)
-            begin(1, 0, 1)
+            begin_other(1, 0)
     with jax.named_scope("z_steps"):
         allow_rest()
         post(piece(0), ZP, 1).start()
@@ -195,22 +229,30 @@
         post(piece(2), ZM, 1).start()
         post(piece(-2), FORE, 1).start()
     with jax.named_scope("own"):
-        @pl.when(even)
-        def _():
-            begin(1, 2)
-
         @pl.when(jnp.logical_not(even))
         def _():
-            begin(0, 0, 1, 2)
-            begin(1, 0, 1, 2)
-
-        for i in range(len(OTHER)):
-            for lane in range(2):
-                second(lane, i, s).start()
+            for order in range(2):
+                begin(order, 0, 1)
+                begin_other(order, 0)
+
+        for order in range(2):
+            begin(order, 2)
+            begin_other(order, 1)
     with jax.named_scope("mate_own"):
         allow(MATE)
         for k in range(2):
             across(k, s, 0, CHUNKS).start()
+
+    def on(planes):
+        return sum(jnp.where(z == k, 1, 0) for k in planes) > 0
+
+    def direct(lane, p):
+        left = [k for k in range(Z) if LEFT[lane][k] > p]
+        return jnp.logical_not(on(left)) if left else z >= 0
+
+    def about(lane, p):
+        left = [(k + 4) % Z for k in range(Z) if LEFT[lane][k] > p]
+        return on(left) if left else z < 0
 
     def own_arrived(i):
         with jax.named_scope(f"half_a{i}"):
@@ -219,21 +261,24 @@
                 first(lane, i, shard).wait_recv()
                 for p, (lo, n) in enumerate(PASSED):
                     if GROUPS[i][0] <= lo < sum(GROUPS[i]):
-                        if lane == 0 and p < SHIFT:
-                            @pl.when(z < 6)
+                        if p < MOST:
+                            @pl.when(direct(lane, p))
                             def _():
-                                passed(0, p, shard, 3).start()
+                                passed(lane, p, shard, 3 + MOST * lane + p).start()
                         else:
                             passed(lane, p, shard).start()
                 across(lane, shard, *GROUPS[i]).start()
 
     def other_arrived(i):
         with jax.named_scope(f"half_b{i}"):
-            copy(0, s, 0, 2 * OTHER[i][1], MATE, core_sem.at[0], second_recv.at[i]).wait_recv()
-            if i < SHIFT:
-                @pl.when(jnp.logical_and(z >= 2, z < 4))
-                def _():
-                    copy(0, arriving(1, 1), *PASSED[0], BACK, ici_send.at[4], passed_recv.at[0, 0]).start()
+            ref = gate.at[rows(0, OTHER[i][1]), 0 : 2 * WIDE]
+            pltpu.make_async_remote_copy(ref, ref, core_sem.at[0], second_recv.at[i], device_id=near[MATE], device_id_type=MESH).wait_recv()
+            for lane in range(2):
+                for p, (lo, n) in enumerate(PASSED[:MOST]):
+                    if OTHER[i][0] <= lo < sum(OTHER[i]):
+                        @pl.when(about(lane, p))
+                        def _():
+                            copy(lane, arriving(1 - lane, 1), lo, n, lanes[1 - lane], ici_send.at[3 + 2 * MOST + p], passed_recv.at[lane, p]).start()
             for lane in range(2):
                 across(1 - lane, arriving(lane, 1), *OTHER[i]).start()
 
@@ -264,17 +309,18 @@
         own_arrived(1)
         other_arrived(0)
         own_arrived(2)
-        other_arrived(1)
 
     @pl.when(even)
     def _():
         arrivals()
         router_rest()
+        other_arrived(1)
 
     @pl.when(jnp.logical_not(even))
     def _():
         router_rest()
         arrivals()
+        other_arrived(1)
 
     with jax.named_scope("router_end"):
         landed(ring.at[1 - c], 8)
@@ -290,7 +336,7 @@
         lax.fori_loop(0, Y * X, lay, 0)
         router[...] = flat[...].astype(jnp.bfloat16)
     order = [(lane, p) for p in range(len(PASSED)) for lane in range(2)]
-    order = order[SHIFT:] + order[:SHIFT]
+    order = order[2 * MOST :] + order[: 2 * MOST]
     for lane, p in order:
         with jax.named_scope(f"passed{p}_{lane}"):
             shard = arriving(lane, 2)
@@ -300,15 +346,13 @@
     with jax.named_scope("finish"):
         sent(gate.at[:, 0 : 2 * WIDE], ici_send.at[0])
         sent(gate.at[:, 0 : 2 * WIDE], ici_send.at[1])
-        if SHIFT:
-            n = PASSED[0][1] * ROWS
-            sent(gate.at[0 : D_EXPERT - n // 2, 0 : 2 * WIDE], ici_send.at[2])
-            for i, when in ((3, z < 6), (4, jnp.logical_and(z >= 2, z < 4))):
+        sent(gate.at[0 : D_EXPERT - sum(n for _, n in PASSED[:MOST]) * ROWS, 0 : 2 * WIDE], ici_send.at[2])
+        for p, (_, n) in enumerate(PASSED[:MOST]):
+            for i, when in (
+                (3 + p, direct(0, p)), (3 + MOST + p, direct(1, p)), (3 + 2 * MOST + p, jnp.logical_or(about(0, p), about(1, p)))):
                 @pl.when(when)
                 def _():
-                    sent(gate.at[0:n, 0:WIDE], ici_send.at[i])
-        else:
-            sent(gate.at[:, 0 : 2 * WIDE], ici_send.at[2])
+                    sent(gate.at[0 : n * ROWS, 0:WIDE], ici_send.at[i])
         sent(ring.at[c, y, x, 0:7], r_send.at[0])
         sent(ring.at[c, y, 0:3], r_send.at[1])
         sent(ring.at[c, 0:7], r_send.at[2])
@@ -352,7 +396,7 @@
             dma((2, len(GROUPS))),
             dma((len(OTHER),)),
             dma((2, len(PASSED))),
-            dma((5,)),
+            dma((3 + 3 * MOST,)),
             dma((2,)),
             dma((4,)),
             dma((9,)),

time: 85.9 us -> 83.3 us (0.970)
  the two profiles are of different devices: /device:TPU:127 before, /device:TPU:121 now
where the time goes in v3:
time: 83.3 us; the launch traced here: 83.2 us
  Pallas kernels  81.9 us (98%)
  between operations  1.29 us (2%)
    pallas_call x1, Pallas kernels, local(): pl.pallas_call(kernel, out_shape=outs, in_specs=[hbm] * 6 + [vmem], out_s...  78.5 us
    pallas_call x1, Pallas kernels, local(): pl.pallas_call(store, out_shape=outs, in_specs=[vmem] * 3, out_specs=(hbm...  3.45 us

profile of v3, /device:TPU:121, one launch (start us, length us, event | category | flops | bytes accessed | tf_op | source)
XLA Modules:
  0.0 83.2 jit_solution(7555365613178725152)
XLA Ops:
  1.3 78.5 %mix_and_gather.1 = (bf16[1024,2048]{1,0:T(8,128)(2,1)S(1)}, bf16[1024,2048]{1,0:T(8,128)(2,1)S(1)}, bf16[64,2048]{1,0:T(8,128)(2,1)S(1)}) custom-call(f32[1,256,1024]{2,1,0:T(8,128)} %wg.1, f32[1,256,1024]{2,1,0:T(8,128)} %ag.1, f32[1,256,1024]{2,1,0:T(8,128)} %wu.1, f32[1,256,1024]{2,1,0:T(8,128)} %au.1, f32[1,256]{1,0:T(1,128)} %bitcast.7, ...), custom_call_target="tpu_custom_call" | custom-call | tf_op jit(solution)/shard_map/mix_and_gather/pallas_call | solution.py:383
  79.7 3.5 %store.1 = (bf16[1024,2048]{1,0:T(8,128)(2,1)}, bf16[1024,2048]{1,0:T(8,128)(2,1)}, bf16[64,2048]{1,0:T(8,128)(2,1)}) custom-call(bf16[1024,2048]{1,0:T(8,128)(2,1)S(1)} %get-tuple-element.9.gate, bf16[1024,2048]{1,0:T(8,128)(2,1)S(1)} %get-tuple-element.10.up, bf16[64,2048]{1,0:T(8,128)(2,1)S(1)} %get-tuple-element.11.router), custom_call_target="tpu_custom_call" | custom-call | tf_op jit(solution)/shard_map/store/pallas_call | solution.py:410

commit v4 on v3

--- a/solution.py
+++ b/solution.py
@@ -11,15 +11,16 @@
 ROWS = 128
 CHUNKS = D_EXPERT // ROWS
 X, Y, Z = 4, 8, 8
-FORE, BACK, MATE, ZP, ZM, XP, XM, YP, YM = range(9)
-OPPOSITE = (BACK, FORE, MATE, ZM, ZP, XM, XP, YM, YP)
+FORE, BACK, MATE, ZP, ZM, XP, XM, YP, YM, FORE_MATE, BACK_MATE = range(11)
+OPPOSITE = (BACK, FORE, MATE, ZM, ZP, XM, XP, YM, YP, BACK_MATE, FORE_MATE)
+TWICE = 32
 GROUPS = ((0, 1), (1, 3), (4, 4))
 OTHER = ((0, 2), (2, 6))
-PASSED = ((0, 1), (1, 1), (2, 2), (4, 2), (6, 1), (7, 1))
+PASSED = ((0, 128), (128, 128), (256, 256), (512, 256), (768, 128), (896, 128 - TWICE), (1024 - TWICE, TWICE))
 LEFT = (0, 0, 0, 0, 0, 0, 2, 0), (2, 0, 0, 0, 1, 0, 0, 0)
 MOST = 2
+LAST = len(PASSED) - 1
 LATE = 6
-PARTS = 4
 
 
 def kernel(wg, ag, wu, au, rw_any, gain_any, mix, gate, up, router, held, load_sem, small, small_sem, ring, flat,
@@ -37,11 +38,11 @@
     for g in range(len(GROUPS)):
         for k in (1, 0):
             for i, ref in enumerate(((wg, ag), (wu, au))[k]):
-                pltpu.make_async_copy(ref.at[0, :, columns_of(g)], held.at[2 * k + i, :, columns_of(g)], load_sem.at[k, g]).start()
-
-    def loaded(k, g):
-        ref = held.at[2 * k : 2 * k + 2, :, columns_of(g)]
-        pltpu.make_async_copy(ref, ref, load_sem.at[k, g]).wait()
+                pltpu.make_async_copy(ref.at[0, :, columns_of(g)], held.at[2 * k + i, :, columns_of(g)], load_sem.at[g]).start()
+
+    def loaded(g):
+        ref = held.at[:, :, columns_of(g)]
+        pltpu.make_async_copy(ref, ref, load_sem.at[g]).wait()
 
     def place(dx=0, dy=0, dz=0, dc=0):
         return (x + dx) & (X - 1), (y + dy) & (Y - 1), (z + dz) & (Z - 1), (c + dc) & 1
@@ -53,14 +54,15 @@
         order = (p[2] << 7) + (p[1] << 4) + (p[0] << 2) + 2 - 2 * p[3]
         return jnp.where(order == 2, (LATE << 7) - 1, order)
 
-    places = [place(dz=2), place(dz=-2), place(dc=1), place(dz=1), place(dz=-1), place(dx=1), place(dx=-1), place(dy=1), place(dy=-1)]
+    places = [place(dz=2), place(dz=-2), place(dc=1), place(dz=1), place(dz=-1), place(dx=1), place(dx=-1), place(dy=1), place(dy=-1),
+              place(dz=2, dc=1), place(dz=-2, dc=1)]
     near = [device(p) for p in places]
     own_rank = rank(place())
     earlier = [rank(p) < own_rank for p in places]
     lanes = (FORE, BACK)
 
     barrier = pltpu.get_barrier_semaphore()
-    for k in range(9):
+    for k in range(11):
         @pl.when(jnp.logical_not(earlier[k]))
         def _():
             pl.semaphore_signal(barrier, inc=1, device_id=near[k], device_id_type=MESH)
@@ -71,7 +73,7 @@
         def _():
             pl.semaphore_wait(barrier, before)
 
-        for k in range(9):
+        for k in range(11):
             @pl.when(earlier[k])
             def _():
                 pl.semaphore_signal(ready.at[min(OPPOSITE[k], ZP)], inc=1, device_id=near[k], device_id_type=MESH)
@@ -82,7 +84,7 @@
             pl.semaphore_wait(ready.at[k], 1)
 
     def allow_rest():
-        after = sum(1 - earlier[k].astype(jnp.int32) for k in range(ZP, 9))
+        after = sum(1 - earlier[k].astype(jnp.int32) for k in range(ZP, 11))
 
         @pl.when(after > 0)
         def _():
@@ -101,21 +103,28 @@
         fresh = share * held[2 * k, :, rows(j)] + rest * held[2 * k + 1, :, rows(j)]
         (gate, up)[k][rows(j), columns(s)] = fresh.T.astype(jnp.bfloat16)
 
-    def copy(k, shard, j, n, to, send, recv):
-        ref = (gate, up)[k].at[rows(j, n), columns(shard)]
+    def copy(k, shard, lo, n, to, send, recv):
+        ref = (gate, up)[k].at[pl.ds(lo, n), columns(shard)]
         return pltpu.make_async_remote_copy(ref, ref, send, recv, device_id=near[to], device_id_type=MESH)
 
-    def first(lane, i, shard):
-        return copy(lane, shard, *GROUPS[i], lanes[lane], ici_send.at[lane], first_recv.at[lane, i])
-
-    def second(lane, i, shard):
-        return copy(1 - lane, shard, *OTHER[i], lanes[lane], ici_send.at[lane], second_recv.at[i])
-
-    def passed(lane, i, shard, send=2):
-        return copy(lane, shard, *PASSED[i], lanes[lane], ici_send.at[send], passed_recv.at[lane, i])
-
-    def across(k, shard, j, n=1):
-        return copy(k, shard, j, n, MATE, core_sem.at[0], core_sem.at[1])
+    def chunks(j, n):
+        return j * ROWS, n * ROWS
+
+    def first(lane, i):
+        return copy(lane, s, *chunks(*GROUPS[i]), lanes[lane], ici_send.at[0], first_recv.at[i])
+
+    def second(lane, i):
+        return copy(1 - lane, s, *chunks(*OTHER[i]), lanes[lane], ici_send.at[0], second_recv.at[i])
+
+    def passed(lane, p, shard, send=0):
+        return copy(lane, shard, *PASSED[p], lanes[lane], ici_send.at[send], passed_recv.at[p])
+
+    def across(k, shard, lo, n):
+        return copy(k, shard, lo, n, MATE, core_sem.at[0], core_sem.at[1])
+
+    def arrived(n, sem):
+        ref = gate.at[0:n, 0 : 2 * WIDE]
+        pltpu.make_async_remote_copy(ref, ref, core_sem.at[0], sem, device_id=near[MATE], device_id_type=MESH).wait_recv()
 
     def arriving(lane, far):
         return ((z_hi + (4 - far if lane == 0 else far)) & 3) * 2 + c
@@ -125,7 +134,7 @@
 
     def post(ref, to, i):
         return pltpu.make_async_remote_copy(
-            ref, ref, r_send.at[(0, 0, 1, 1, 2, 2, 2, 2, 3)[i]], r_recv.at[i], device_id=near[to], device_id_type=MESH)
+            ref, ref, r_send.at[min(i // 2, 1)], r_recv.at[i], device_id=near[to], device_id_type=MESH)
 
     def piece(k):
         return ring.at[c, y, x, (z + k) & (Z - 1)]
@@ -152,19 +161,18 @@
         post(piece(0), lanes[lane], 0).start()
 
     def begin(order, *which):
-        in_turn(order, lambda lane: [first(lane, i, s).start() for i in which])
+        in_turn(order, lambda lane: [first(lane, i).start() for i in which])
 
     def begin_other(order, *which):
-        in_turn(order, lambda lane: [second(lane, i, s).start() for i in which])
+        in_turn(order, lambda lane: [second(lane, i).start() for i in which])
 
     both = jnp.logical_and(even, z >= 6)
     one = jnp.logical_and(even, z < 6)
 
     with jax.named_scope("first_chunk"):
         answer()
-        loaded(1, 0)
+        loaded(0)
         compute(1, 0)
-        loaded(0, 0)
         compute(0, 0)
     with jax.named_scope("admit_first"):
         in_turn(0, lambda lane: allow(lanes[lane]))
@@ -183,8 +191,7 @@
             return 0
 
         def more_of(g):
-            for k in (1, 0):
-                loaded(k, g)
+            loaded(g)
             lax.fori_loop(GROUPS[g][0], sum(GROUPS[g]), more, 0)
 
         more_of(1)
@@ -241,7 +248,7 @@
     with jax.named_scope("mate_own"):
         allow(MATE)
         for k in range(2):
-            across(k, s, 0, CHUNKS).start()
+            across(k, s, 0, D_EXPERT).start()
 
     def on(planes):
         return sum(jnp.where(z == k, 1, 0) for k in planes) > 0
@@ -254,33 +261,40 @@
         left = [(k + 4) % Z for k in range(Z) if LEFT[lane][k] > p]
         return on(left) if left else z < 0
 
+    odd = jnp.logical_not(even)
+
     def own_arrived(i):
         with jax.named_scope(f"half_a{i}"):
+            start, length = chunks(*GROUPS[i])
+            arrived(length, first_recv.at[i])
             for lane in range(2):
                 shard = arriving(lane, 1)
-                first(lane, i, shard).wait_recv()
                 for p, (lo, n) in enumerate(PASSED):
-                    if GROUPS[i][0] <= lo < sum(GROUPS[i]):
+                    if start <= lo < start + length:
                         if p < MOST:
                             @pl.when(direct(lane, p))
                             def _():
-                                passed(lane, p, shard, 3 + MOST * lane + p).start()
+                                passed(lane, p, shard, 1 + MOST * lane + p).start()
                         else:
                             passed(lane, p, shard).start()
-                across(lane, shard, *GROUPS[i]).start()
+                        if p == LAST:
+                            @pl.when(odd)
+                            def _():
+                                copy(lane, shard, lo, n, (FORE_MATE, BACK_MATE)[lane], ici_send.at[1 + 3 * MOST], passed_recv.at[LAST + 1]).start()
+                across(lane, shard, start, length).start()
 
     def other_arrived(i):
         with jax.named_scope(f"half_b{i}"):
-            ref = gate.at[rows(0, OTHER[i][1]), 0 : 2 * WIDE]
-            pltpu.make_async_remote_copy(ref, ref, core_sem.at[0], second_recv.at[i], device_id=near[MATE], device_id_type=MESH).wait_recv()
+            start, length = chunks(*OTHER[i])
+            arrived(length, second_recv.at[i])
             for lane in range(2):
                 for p, (lo, n) in enumerate(PASSED[:MOST]):
-                    if OTHER[i][0] <= lo < sum(OTHER[i]):
+                    if start <= lo < start + length:
                         @pl.when(about(lane, p))
                         def _():
-                            copy(lane, arriving(1 - lane, 1), lo, n, lanes[1 - lane], ici_send.at[3 + 2 * MOST + p], passed_recv.at[lane, p]).start()
+                            copy(lane, arriving(1 - lane, 1), lo, n, lanes[1 - lane], ici_send.at[1 + 2 * MOST + p], passed_recv.at[p]).start()
             for lane in range(2):
-                across(1 - lane, arriving(lane, 1), *OTHER[i]).start()
+                across(1 - lane, arriving(lane, 1), start, length).start()
 
     def router_rest():
         with jax.named_scope("router_x1"):
@@ -335,39 +349,47 @@
 
         lax.fori_loop(0, Y * X, lay, 0)
         router[...] = flat[...].astype(jnp.bfloat16)
-    order = [(lane, p) for p in range(len(PASSED)) for lane in range(2)]
-    order = order[2 * MOST :] + order[: 2 * MOST]
-    for lane, p in order:
-        with jax.named_scope(f"passed{p}_{lane}"):
-            shard = arriving(lane, 2)
-            passed(lane, p, shard).wait_recv()
-            across(lane, shard, *PASSED[p]).start()
+    for p, (lo, n) in enumerate(PASSED):
+        with jax.named_scope(f"passed{p}"):
+            arrived(n, passed_recv.at[p])
+            if p < LAST:
+                for lane in range(2):
+                    across(lane, arriving(lane, 2), lo, n).start()
 
     with jax.named_scope("finish"):
-        sent(gate.at[:, 0 : 2 * WIDE], ici_send.at[0])
-        sent(gate.at[:, 0 : 2 * WIDE], ici_send.at[1])
-        sent(gate.at[0 : D_EXPERT - sum(n for _, n in PASSED[:MOST]) * ROWS, 0 : 2 * WIDE], ici_send.at[2])
+        @pl.when(even)
+        def _():
+            for lane in range(2):
+                across(lane, arriving(lane, 2), *PASSED[LAST]).start()
+
+        always = 4 * D_EXPERT + 2 * sum(n for _, n in PASSED[MOST:])
+        sent(gate.at[0 : always // SHARDS, :], ici_send.at[0])
         for p, (_, n) in enumerate(PASSED[:MOST]):
-            for i, when in (
-                (3 + p, direct(0, p)), (3 + MOST + p, direct(1, p)), (3 + 2 * MOST + p, jnp.logical_or(about(0, p), about(1, p)))):
+            for i, when in ((0, direct(0, p)), (1, direct(1, p)), (2, jnp.logical_or(about(0, p), about(1, p)))):
                 @pl.when(when)
                 def _():
-                    sent(gate.at[0 : n * ROWS, 0:WIDE], ici_send.at[i])
+                    sent(gate.at[0:n, 0:WIDE], ici_send.at[1 + MOST * i + p])
         sent(ring.at[c, y, x, 0:7], r_send.at[0])
-        sent(ring.at[c, y, 0:3], r_send.at[1])
-        sent(ring.at[c, 0:7], r_send.at[2])
-        sent(ring.at[c], r_send.at[3])
-        sent(gate, core_sem.at[0])
-        pltpu.make_async_remote_copy(gate, gate, core_sem.at[0], core_sem.at[1], device_id=near[MATE], device_id_type=MESH).wait_recv()
+        sent(held.at[0, 0:168, 0:768], r_send.at[1])
+
+        def swapped(ref):
+            sent(ref, core_sem.at[0])
+            pltpu.make_async_remote_copy(ref, ref, core_sem.at[0], core_sem.at[1], device_id=near[MATE], device_id_type=MESH).wait_recv()
+
+        @pl.when(odd)
+        def _():
+            sent(gate.at[0:TWICE, 0 : 2 * WIDE], ici_send.at[1 + 3 * MOST])
+            arrived(TWICE, passed_recv.at[LAST + 1])
+            swapped(gate.at[0 : D_EXPERT - 2 * TWICE // SHARDS, :])
+
+        @pl.when(even)
+        def _():
+            swapped(gate)
 
 
 def store(gate, up, router, gate_out, up_out, router_out, sem):
-    copies = []
-    for k, (a, b) in enumerate(((gate, gate_out), (up, up_out))):
-        for i in range(PARTS):
-            rows = pl.ds(i * (D_EXPERT // PARTS), D_EXPERT // PARTS)
-            copies.append(pltpu.make_async_copy(a.at[rows], b.at[rows], sem.at[k, i]))
-    copies.append(pltpu.make_async_copy(router, router_out, sem.at[2, 0]))
+    copies = [pltpu.make_async_copy(a, b, sem.at[i])
+              for i, (a, b) in enumerate(((gate, gate_out), (up, up_out), (router, router_out)))]
     for copy in copies:
         copy.start()
     for copy in copies:
@@ -387,18 +409,18 @@
         out_specs=(vmem,) * 3,
         scratch_shapes=[
             pltpu.VMEM((4, WIDE, D_EXPERT), jnp.float32),
-            dma((2, len(GROUPS))),
+            dma((len(GROUPS),)),
             pltpu.VMEM((2, 1, WIDE), jnp.float32),
             dma,
             pltpu.VMEM((2, Y, X, Z, 1, WIDE), jnp.float32),
             pltpu.VMEM((EXPERTS, D_MODEL), jnp.float32),
             pltpu.SemaphoreType.REGULAR((4,)),
-            dma((2, len(GROUPS))),
+            dma((len(GROUPS),)),
             dma((len(OTHER),)),
-            dma((2, len(PASSED))),
-            dma((3 + 3 * MOST,)),
+            dma((len(PASSED) + 1,)),
+            dma((2 + 3 * MOST,)),
             dma((2,)),
-            dma((4,)),
+            dma((2,)),
             dma((9,)),
         ],
         compiler_params=pltpu.CompilerParams(
@@ -412,7 +434,7 @@
         out_shape=outs,
         in_specs=[vmem] * 3,
         out_specs=(hbm,) * 3,
-        scratch_shapes=[dma((3, PARTS))],
+        scratch_shapes=[dma((3,))],
         compiler_params=pltpu.CompilerParams(vmem_limit_bytes=2**20),
         name="store",
     )(*gathered)

time: 83.3 us -> 82.5 us (level)
  the two profiles are of different devices: /device:TPU:121 before, /device:TPU:433 now
where the time goes in v4:
time: 82.5 us; the launch traced here: 82.4 us
  Pallas kernels  81.1 us (98%)
  between operations  1.29 us (2%)
    pallas_call x1, Pallas kernels, local(): pl.pallas_call(kernel, out_shape=outs, in_specs=[hbm] * 6 + [vmem], out_s...  77.7 us
    pallas_call x1, Pallas kernels, local(): pl.pallas_call(store, out_shape=outs, in_specs=[vmem] * 3, out_specs=(hbm...  3.42 us

profile of v4, /device:TPU:433, one launch (start us, length us, event | category | flops | bytes accessed | tf_op | source)
XLA Modules:
  0.0 82.4 jit_solution(9193560581147134663)
XLA Ops:
  1.3 77.7 %mix_and_gather.1 = (bf16[1024,2048]{1,0:T(8,128)(2,1)S(1)}, bf16[1024,2048]{1,0:T(8,128)(2,1)S(1)}, bf16[64,2048]{1,0:T(8,128)(2,1)S(1)}) custom-call(f32[1,256,1024]{2,1,0:T(8,128)} %wg.1, f32[1,256,1024]{2,1,0:T(8,128)} %ag.1, f32[1,256,1024]{2,1,0:T(8,128)} %wu.1, f32[1,256,1024]{2,1,0:T(8,128)} %au.1, f32[1,256]{1,0:T(1,128)} %bitcast.7, ...), custom_call_target="tpu_custom_call" | custom-call | tf_op jit(solution)/shard_map/mix_and_gather/pallas_call | solution.py:405
  79.0 3.4 %store.1 = (bf16[1024,2048]{1,0:T(8,128)(2,1)}, bf16[1024,2048]{1,0:T(8,128)(2,1)}, bf16[64,2048]{1,0:T(8,128)(2,1)}) custom-call(bf16[1024,2048]{1,0:T(8,128)(2,1)S(1)} %get-tuple-element.9.gate, bf16[1024,2048]{1,0:T(8,128)(2,1)S(1)} %get-tuple-element.10.up, bf16[64,2048]{1,0:T(8,128)(2,1)S(1)} %get-tuple-element.11.router), custom_call_target="tpu_custom_call" | custom-call | tf_op jit(solution)/shard_map/store/pallas_call | solution.py:432

commit v5 on v4

--- a/solution.py
+++ b/solution.py
@@ -16,10 +16,10 @@
 TWICE = 32
 GROUPS = ((0, 1), (1, 3), (4, 4))
 OTHER = ((0, 2), (2, 6))
-PASSED = ((0, 128), (128, 128), (256, 256), (512, 256), (768, 128), (896, 128 - TWICE), (1024 - TWICE, TWICE))
-LEFT = (0, 0, 0, 0, 0, 0, 2, 0), (2, 0, 0, 0, 1, 0, 0, 0)
-MOST = 2
+STEP, MOST = 64, 4
+PASSED = ((MOST * STEP, 256), (512, 256), (768, 128), (896, 128 - TWICE), (1024 - TWICE, TWICE))
 LAST = len(PASSED) - 1
+LEFT = (0, 0, 0, 0, 0, 0, 4, 0), (3, 0, 0, 0, 2, 1, 0, 0)
 LATE = 6
 
 
@@ -116,8 +116,11 @@
     def second(lane, i):
         return copy(1 - lane, s, *chunks(*OTHER[i]), lanes[lane], ici_send.at[0], second_recv.at[i])
 
-    def passed(lane, p, shard, send=0):
-        return copy(lane, shard, *PASSED[p], lanes[lane], ici_send.at[send], passed_recv.at[p])
+    def passed(lane, p, shard):
+        return copy(lane, shard, *PASSED[p], lanes[lane], ici_send.at[0], passed_recv.at[p])
+
+    def shared(lane, i, shard, to):
+        return copy(lane, shard, i * STEP, STEP, to, ici_send.at[1], passed_recv.at[LAST + 2])
 
     def across(k, shard, lo, n):
         return copy(k, shard, lo, n, MATE, core_sem.at[0], core_sem.at[1])
@@ -250,16 +253,11 @@
         for k in range(2):
             across(k, s, 0, D_EXPERT).start()
 
-    def on(planes):
-        return sum(jnp.where(z == k, 1, 0) for k in planes) > 0
-
-    def direct(lane, p):
-        left = [k for k in range(Z) if LEFT[lane][k] > p]
-        return jnp.logical_not(on(left)) if left else z >= 0
-
-    def about(lane, p):
-        left = [(k + 4) % Z for k in range(Z) if LEFT[lane][k] > p]
-        return on(left) if left else z < 0
+    def at_plane(table):
+        return sum(jnp.where(z == k, v, 0) for k, v in enumerate(table) if v) + jnp.where(z < 0, 1, 0)
+
+    left = [at_plane(LEFT[lane]) for lane in range(2)]
+    taken = [at_plane([LEFT[lane][(k + 4) % Z] for k in range(Z)]) for lane in range(2)]
 
     odd = jnp.logical_not(even)
 
@@ -269,18 +267,18 @@
             arrived(length, first_recv.at[i])
             for lane in range(2):
                 shard = arriving(lane, 1)
+                for j in range(MOST):
+                    if start <= j * STEP < start + length:
+                        @pl.when(j >= left[lane])
+                        def _():
+                            shared(lane, j, shard, lanes[lane]).start()
                 for p, (lo, n) in enumerate(PASSED):
                     if start <= lo < start + length:
-                        if p < MOST:
-                            @pl.when(direct(lane, p))
-                            def _():
-                                passed(lane, p, shard, 1 + MOST * lane + p).start()
-                        else:
-                            passed(lane, p, shard).start()
+                        passed(lane, p, shard).start()
                         if p == LAST:
                             @pl.when(odd)
                             def _():
-                                copy(lane, shard, lo, n, (FORE_MATE, BACK_MATE)[lane], ici_send.at[1 + 3 * MOST], passed_recv.at[LAST + 1]).start()
+                                copy(lane, shard, lo, n, (FORE_MATE, BACK_MATE)[lane], ici_send.at[2], passed_recv.at[LAST + 1]).start()
                 across(lane, shard, start, length).start()
 
     def other_arrived(i):
@@ -288,11 +286,11 @@
             start, length = chunks(*OTHER[i])
             arrived(length, second_recv.at[i])
             for lane in range(2):
-                for p, (lo, n) in enumerate(PASSED[:MOST]):
-                    if start <= lo < start + length:
-                        @pl.when(about(lane, p))
+                for j in range(MOST):
+                    if start <= j * STEP < start + length and max(LEFT[lane]) > j:
+                        @pl.when(j < taken[lane])
                         def _():
-                            copy(lane, arriving(1 - lane, 1), lo, n, lanes[1 - lane], ici_send.at[1 + 2 * MOST + p], passed_recv.at[p]).start()
+                            shared(lane, j, arriving(1 - lane, 1), lanes[1 - lane]).start()
             for lane in range(2):
                 across(1 - lane, arriving(lane, 1), start, length).start()
 
@@ -349,26 +347,31 @@
 
         lax.fori_loop(0, Y * X, lay, 0)
         router[...] = flat[...].astype(jnp.bfloat16)
+    def passed_across(lo, n):
+        for lane in range(2):
+            across(lane, arriving(lane, 2), lo, n).start()
+
+    with jax.named_scope("shared"):
+        arrived(MOST * STEP, passed_recv.at[LAST + 2])
+        passed_across(0, MOST * STEP)
     for p, (lo, n) in enumerate(PASSED):
         with jax.named_scope(f"passed{p}"):
             arrived(n, passed_recv.at[p])
             if p < LAST:
-                for lane in range(2):
-                    across(lane, arriving(lane, 2), lo, n).start()
+                passed_across(lo, n)
 
     with jax.named_scope("finish"):
         @pl.when(even)
         def _():
-            for lane in range(2):
-                across(lane, arriving(lane, 2), *PASSED[LAST]).start()
-
-        always = 4 * D_EXPERT + 2 * sum(n for _, n in PASSED[MOST:])
+            passed_across(*PASSED[LAST])
+
+        always = 4 * D_EXPERT + 2 * (D_EXPERT - MOST * STEP)
         sent(gate.at[0 : always // SHARDS, :], ici_send.at[0])
-        for p, (_, n) in enumerate(PASSED[:MOST]):
-            for i, when in ((0, direct(0, p)), (1, direct(1, p)), (2, jnp.logical_or(about(0, p), about(1, p)))):
-                @pl.when(when)
-                def _():
-                    sent(gate.at[0:n, 0:WIDE], ici_send.at[1 + MOST * i + p])
+        times = 2 * MOST + sum(taken) - sum(left)
+        for t in sorted({2 * MOST + sum(LEFT[lane][(k + 4) % Z] - LEFT[lane][k] for lane in range(2)) for k in range(Z)}):
+            @pl.when(times == t)
+            def _():
+                sent(gate.at[0 : STEP * t // 2, 0 : 2 * WIDE], ici_send.at[1])
         sent(ring.at[c, y, x, 0:7], r_send.at[0])
         sent(held.at[0, 0:168, 0:768], r_send.at[1])
 
@@ -378,7 +381,7 @@
 
         @pl.when(odd)
         def _():
-            sent(gate.at[0:TWICE, 0 : 2 * WIDE], ici_send.at[1 + 3 * MOST])
+            sent(gate.at[0:TWICE, 0 : 2 * WIDE], ici_send.at[2])
             arrived(TWICE, passed_recv.at[LAST + 1])
             swapped(gate.at[0 : D_EXPERT - 2 * TWICE // SHARDS, :])
 
@@ -417,8 +420,8 @@
             pltpu.SemaphoreType.REGULAR((4,)),
             dma((len(GROUPS),)),
             dma((len(OTHER),)),
-            dma((len(PASSED) + 1,)),
-            dma((2 + 3 * MOST,)),
+            dma((len(PASSED) + 2,)),
+            dma((3,)),
             dma((2,)),
             dma((2,)),
             dma((9,)),

time: 82.5 us -> 82.4 us (level)
  the two profiles are of different devices: /device:TPU:433 before, /device:TPU:121 now
where the time goes in v5:
time: 82.4 us; the launch traced here: 82.3 us
  Pallas kernels  81 us (98%)
  between operations  1.29 us (2%)
    pallas_call x1, Pallas kernels, local(): pl.pallas_call(kernel, out_shape=outs, in_specs=[hbm] * 6 + [vmem], out_s...  77.6 us
    pallas_call x1, Pallas kernels, local(): pl.pallas_call(store, out_shape=outs, in_specs=[vmem] * 3, out_specs=(hbm...  3.42 us

profile of v5, /device:TPU:121, one launch (start us, length us, event | category | flops | bytes accessed | tf_op | source)
XLA Modules:
  0.0 82.3 jit_solution(10572489724459756815)
XLA Ops:
  1.3 77.6 %mix_and_gather.1 = (bf16[1024,2048]{1,0:T(8,128)(2,1)S(1)}, bf16[1024,2048]{1,0:T(8,128)(2,1)S(1)}, bf16[64,2048]{1,0:T(8,128)(2,1)S(1)}) custom-call(f32[1,256,1024]{2,1,0:T(8,128)} %wg.1, f32[1,256,1024]{2,1,0:T(8,128)} %ag.1, f32[1,256,1024]{2,1,0:T(8,128)} %wu.1, f32[1,256,1024]{2,1,0:T(8,128)} %au.1, f32[1,256]{1,0:T(1,128)} %bitcast.7, ...), custom_call_target="tpu_custom_call" | custom-call | tf_op jit(solution)/shard_map/mix_and_gather/pallas_call | solution.py:408
  78.9 3.4 %store.1 = (bf16[1024,2048]{1,0:T(8,128)(2,1)}, bf16[1024,2048]{1,0:T(8,128)(2,1)}, bf16[64,2048]{1,0:T(8,128)(2,1)}) custom-call(bf16[1024,2048]{1,0:T(8,128)(2,1)S(1)} %get-tuple-element.9.gate, bf16[1024,2048]{1,0:T(8,128)(2,1)S(1)} %get-tuple-element.10.up, bf16[64,2048]{1,0:T(8,128)(2,1)S(1)} %get-tuple-element.11.router), custom_call_target="tpu_custom_call" | custom-call | tf_op jit(solution)/shard_map/store/pallas_call | solution.py:435

commit v6 on v5

--- a/solution.py
+++ b/solution.py
@@ -13,7 +13,7 @@
 X, Y, Z = 4, 8, 8
 FORE, BACK, MATE, ZP, ZM, XP, XM, YP, YM, FORE_MATE, BACK_MATE = range(11)
 OPPOSITE = (BACK, FORE, MATE, ZM, ZP, XM, XP, YM, YP, BACK_MATE, FORE_MATE)
-TWICE = 32
+TWICE = 64
 GROUPS = ((0, 1), (1, 3), (4, 4))
 OTHER = ((0, 2), (2, 6))
 STEP, MOST = 64, 4

time: 82.4 us -> 82.2 us (level)
  no operation moved by 1% of the time
where the time goes in v6:
time: 82.2 us; the launch traced here: 82 us
  Pallas kernels  80.7 us (98%)
  between operations  1.29 us (2%)
    pallas_call x1, Pallas kernels, local(): pl.pallas_call(kernel, out_shape=outs, in_specs=[hbm] * 6 + [vmem], out_s...  77.3 us
    pallas_call x1, Pallas kernels, local(): pl.pallas_call(store, out_shape=outs, in_specs=[vmem] * 3, out_specs=(hbm...  3.42 us

profile of v6, /device:TPU:121, one launch (start us, length us, event | category | flops | bytes accessed | tf_op | source)
XLA Modules:
  0.0 82.0 jit_solution(17840051303102568517)
XLA Ops:
  1.3 77.3 %mix_and_gather.1 = (bf16[1024,2048]{1,0:T(8,128)(2,1)S(1)}, bf16[1024,2048]{1,0:T(8,128)(2,1)S(1)}, bf16[64,2048]{1,0:T(8,128)(2,1)S(1)}) custom-call(f32[1,256,1024]{2,1,0:T(8,128)} %wg.1, f32[1,256,1024]{2,1,0:T(8,128)} %ag.1, f32[1,256,1024]{2,1,0:T(8,128)} %wu.1, f32[1,256,1024]{2,1,0:T(8,128)} %au.1, f32[1,256]{1,0:T(1,128)} %bitcast.7, ...), custom_call_target="tpu_custom_call" | custom-call | tf_op jit(solution)/shard_map/mix_and_gather/pallas_call | solution.py:408
  78.6 3.4 %store.1 = (bf16[1024,2048]{1,0:T(8,128)(2,1)}, bf16[1024,2048]{1,0:T(8,128)(2,1)}, bf16[64,2048]{1,0:T(8,128)(2,1)}) custom-call(bf16[1024,2048]{1,0:T(8,128)(2,1)S(1)} %get-tuple-element.9.gate, bf16[1024,2048]{1,0:T(8,128)(2,1)S(1)} %get-tuple-element.10.up, bf16[64,2048]{1,0:T(8,128)(2,1)S(1)} %get-tuple-element.11.router), custom_call_target="tpu_custom_call" | custom-call | tf_op jit(solution)/shard_map/store/pallas_call | solution.py:435

commit v7 on v6

--- a/solution.py
+++ b/solution.py
@@ -17,7 +17,7 @@
 GROUPS = ((0, 1), (1, 3), (4, 4))
 OTHER = ((0, 2), (2, 6))
 STEP, MOST = 64, 4
-PASSED = ((MOST * STEP, 256), (512, 256), (768, 128), (896, 128 - TWICE), (1024 - TWICE, TWICE))
+PASSED = ((MOST * STEP, 256), (512, 256), (768, 256 - TWICE), (1024 - TWICE, TWICE))
 LAST = len(PASSED) - 1
 LEFT = (0, 0, 0, 0, 0, 0, 4, 0), (3, 0, 0, 0, 2, 1, 0, 0)
 LATE = 6
@@ -111,16 +111,16 @@
         return j * ROWS, n * ROWS
 
     def first(lane, i):
-        return copy(lane, s, *chunks(*GROUPS[i]), lanes[lane], ici_send.at[0], first_recv.at[i])
+        return copy(lane, s, *chunks(*GROUPS[i]), lanes[lane], ici_send, first_recv.at[i])
 
     def second(lane, i):
-        return copy(1 - lane, s, *chunks(*OTHER[i]), lanes[lane], ici_send.at[0], second_recv.at[i])
+        return copy(1 - lane, s, *chunks(*OTHER[i]), lanes[lane], ici_send, second_recv.at[i])
 
     def passed(lane, p, shard):
-        return copy(lane, shard, *PASSED[p], lanes[lane], ici_send.at[0], passed_recv.at[p])
+        return copy(lane, shard, *PASSED[p], lanes[lane], ici_send, passed_recv.at[p])
 
     def shared(lane, i, shard, to):
-        return copy(lane, shard, i * STEP, STEP, to, ici_send.at[1], passed_recv.at[LAST + 2])
+        return copy(lane, shard, i * STEP, STEP, to, ici_send, passed_recv.at[LAST + 2])
 
     def across(k, shard, lo, n):
         return copy(k, shard, lo, n, MATE, core_sem.at[0], core_sem.at[1])
@@ -276,9 +276,9 @@
                     if start <= lo < start + length:
                         passed(lane, p, shard).start()
                         if p == LAST:
-                            @pl.when(odd)
+                            @pl.when(z == (7, 3)[lane])
                             def _():
-                                copy(lane, shard, lo, n, (FORE_MATE, BACK_MATE)[lane], ici_send.at[2], passed_recv.at[LAST + 1]).start()
+                                copy(lane, shard, lo, n, (FORE_MATE, BACK_MATE)[lane], ici_send, passed_recv.at[LAST + 1]).start()
                 across(lane, shard, start, length).start()
 
     def other_arrived(i):
@@ -361,17 +361,20 @@
                 passed_across(lo, n)
 
     with jax.named_scope("finish"):
-        @pl.when(even)
+        twice = z == 1
+
+        @pl.when(jnp.logical_not(twice))
         def _():
             passed_across(*PASSED[LAST])
 
-        always = 4 * D_EXPERT + 2 * (D_EXPERT - MOST * STEP)
-        sent(gate.at[0 : always // SHARDS, :], ici_send.at[0])
-        times = 2 * MOST + sum(taken) - sum(left)
-        for t in sorted({2 * MOST + sum(LEFT[lane][(k + 4) % Z] - LEFT[lane][k] for lane in range(2)) for k in range(Z)}):
-            @pl.when(times == t)
+        def rows_sent(k):
+            shared_rows = STEP * (2 * MOST + sum(LEFT[lane][(k + 4) % Z] - LEFT[lane][k] for lane in range(2)))
+            return 4 * D_EXPERT + 2 * (D_EXPERT - MOST * STEP) + shared_rows + TWICE * (k in (3, 7))
+
+        for n in sorted({rows_sent(k) for k in range(Z)}):
+            @pl.when(at_plane([int(rows_sent(k) == n) for k in range(Z)]) > 0)
             def _():
-                sent(gate.at[0 : STEP * t // 2, 0 : 2 * WIDE], ici_send.at[1])
+                sent(gate.at[0 : n // SHARDS, :], ici_send)
         sent(ring.at[c, y, x, 0:7], r_send.at[0])
         sent(held.at[0, 0:168, 0:768], r_send.at[1])
 
@@ -379,13 +382,12 @@
             sent(ref, core_sem.at[0])
             pltpu.make_async_remote_copy(ref, ref, core_sem.at[0], core_sem.at[1], device_id=near[MATE], device_id_type=MESH).wait_recv()
 
-        @pl.when(odd)
-        def _():
-            sent(gate.at[0:TWICE, 0 : 2 * WIDE], ici_send.at[2])
+        @pl.when(twice)
+        def _():
             arrived(TWICE, passed_recv.at[LAST + 1])
             swapped(gate.at[0 : D_EXPERT - 2 * TWICE // SHARDS, :])
 
-        @pl.when(even)
+        @pl.when(jnp.logical_not(twice))
         def _():
             swapped(gate)
 
@@ -421,7 +423,7 @@
             dma((len(GROUPS),)),
             dma((len(OTHER),)),
             dma((len(PASSED) + 2,)),
-            dma((3,)),
+            dma,
             dma((2,)),
             dma((2,)),
             dma((9,)),

time: 82.2 us -> 82.2 us (level)
  no operation moved by 1% of the time
where the time goes in v7:
time: 82.2 us; the launch traced here: 82.1 us
  Pallas kernels  80.8 us (98%)
  between operations  1.29 us (2%)
    pallas_call x1, Pallas kernels, local(): pl.pallas_call(kernel, out_shape=outs, in_specs=[hbm] * 6 + [vmem], out_s...  77.4 us
    pallas_call x1, Pallas kernels, local(): pl.pallas_call(store, out_shape=outs, in_specs=[vmem] * 3, out_specs=(hbm...  3.42 us

profile of v7, /device:TPU:121, one launch (start us, length us, event | category | flops | bytes accessed | tf_op | source)
XLA Modules:
  0.0 82.1 jit_solution(421615571334458323)
XLA Ops:
  1.3 77.4 %mix_and_gather.1 = (bf16[1024,2048]{1,0:T(8,128)(2,1)S(1)}, bf16[1024,2048]{1,0:T(8,128)(2,1)S(1)}, bf16[64,2048]{1,0:T(8,128)(2,1)S(1)}) custom-call(f32[1,256,1024]{2,1,0:T(8,128)} %wg.1, f32[1,256,1024]{2,1,0:T(8,128)} %ag.1, f32[1,256,1024]{2,1,0:T(8,128)} %wu.1, f32[1,256,1024]{2,1,0:T(8,128)} %au.1, f32[1,256]{1,0:T(1,128)} %bitcast.7, ...), custom_call_target="tpu_custom_call" | custom-call | tf_op jit(solution)/shard_map/mix_and_gather/pallas_call | solution.py:410
  78.6 3.4 %store.1 = (bf16[1024,2048]{1,0:T(8,128)(2,1)}, bf16[1024,2048]{1,0:T(8,128)(2,1)}, bf16[64,2048]{1,0:T(8,128)(2,1)}) custom-call(bf16[1024,2048]{1,0:T(8,128)(2,1)S(1)} %get-tuple-element.9.gate, bf16[1024,2048]{1,0:T(8,128)(2,1)S(1)} %get-tuple-element.10.up, bf16[64,2048]{1,0:T(8,128)(2,1)S(1)} %get-tuple-element.11.router), custom_call_target="tpu_custom_call" | custom-call | tf_op jit(solution)/shard_map/store/pallas_call | solution.py:437

commit v8 on v7

--- a/solution.py
+++ b/solution.py
@@ -17,7 +17,7 @@
 GROUPS = ((0, 1), (1, 3), (4, 4))
 OTHER = ((0, 2), (2, 6))
 STEP, MOST = 64, 4
-PASSED = ((MOST * STEP, 256), (512, 256), (768, 256 - TWICE), (1024 - TWICE, TWICE))
+PASSED = ((MOST * STEP, 256), (512, 256), (768, 128), (896, 128 - TWICE), (1024 - TWICE, TWICE))
 LAST = len(PASSED) - 1
 LEFT = (0, 0, 0, 0, 0, 0, 4, 0), (3, 0, 0, 0, 2, 1, 0, 0)
 LATE = 6
@@ -274,11 +274,21 @@
                             shared(lane, j, shard, lanes[lane]).start()
                 for p, (lo, n) in enumerate(PASSED):
                     if start <= lo < start + length:
-                        passed(lane, p, shard).start()
                         if p == LAST:
-                            @pl.when(z == (7, 3)[lane])
+                            again = copy(lane, shard, lo, n, (FORE_MATE, BACK_MATE)[lane], ici_send, passed_recv.at[LAST + 1])
+                            more = z == (7, 3)[lane]
+
+                            @pl.when(jnp.logical_and(more, c == 0))
                             def _():
-                                copy(lane, shard, lo, n, (FORE_MATE, BACK_MATE)[lane], ici_send, passed_recv.at[LAST + 1]).start()
+                                again.start()
+
+                            passed(lane, p, shard).start()
+
+                            @pl.when(jnp.logical_and(more, c == 1))
+                            def _():
+                                again.start()
+                        else:
+                            passed(lane, p, shard).start()
                 across(lane, shard, start, length).start()
 
     def other_arrived(i):

time: 82.2 us -> 82 us (level)
  no operation moved by 1% of the time
where the time goes in v8:
time: 82 us; the launch traced here: 81.9 us
  Pallas kernels  80.6 us (98%)
  between operations  1.29 us (2%)
    pallas_call x1, Pallas kernels, local(): pl.pallas_call(kernel, out_shape=outs, in_specs=[hbm] * 6 + [vmem], out_s...  77.2 us
    pallas_call x1, Pallas kernels, local(): pl.pallas_call(store, out_shape=outs, in_specs=[vmem] * 3, out_specs=(hbm...  3.42 us

profile of v8, /device:TPU:121, one launch (start us, length us, event | category | flops | bytes accessed | tf_op | source)
XLA Modules:
  0.0 81.9 jit_solution(2958696251083489523)
XLA Ops:
  1.3 77.2 %mix_and_gather.1 = (bf16[1024,2048]{1,0:T(8,128)(2,1)S(1)}, bf16[1024,2048]{1,0:T(8,128)(2,1)S(1)}, bf16[64,2048]{1,0:T(8,128)(2,1)S(1)}) custom-call(f32[1,256,1024]{2,1,0:T(8,128)} %wg.1, f32[1,256,1024]{2,1,0:T(8,128)} %ag.1, f32[1,256,1024]{2,1,0:T(8,128)} %wu.1, f32[1,256,1024]{2,1,0:T(8,128)} %au.1, f32[1,256]{1,0:T(1,128)} %bitcast.7, ...), custom_call_target="tpu_custom_call" | custom-call | tf_op jit(solution)/shard_map/mix_and_gather/pallas_call | solution.py:420
  78.5 3.4 %store.1 = (bf16[1024,2048]{1,0:T(8,128)(2,1)}, bf16[1024,2048]{1,0:T(8,128)(2,1)}, bf16[64,2048]{1,0:T(8,128)(2,1)}) custom-call(bf16[1024,2048]{1,0:T(8,128)(2,1)S(1)} %get-tuple-element.9.gate, bf16[1024,2048]{1,0:T(8,128)(2,1)S(1)} %get-tuple-element.10.up, bf16[64,2048]{1,0:T(8,128)(2,1)S(1)} %get-tuple-element.11.router), custom_call_target="tpu_custom_call" | custom-call | tf_op jit(solution)/shard_map/store/pallas_call | solution.py:447

commit v9 on v8

--- a/solution.py
+++ b/solution.py
@@ -364,29 +364,34 @@
     with jax.named_scope("shared"):
         arrived(MOST * STEP, passed_recv.at[LAST + 2])
         passed_across(0, MOST * STEP)
-    for p, (lo, n) in enumerate(PASSED):
+    for p, (lo, n) in enumerate(PASSED[:LAST]):
         with jax.named_scope(f"passed{p}"):
             arrived(n, passed_recv.at[p])
-            if p < LAST:
-                passed_across(lo, n)
+            passed_across(lo, n)
 
     with jax.named_scope("finish"):
-        twice = z == 1
-
-        @pl.when(jnp.logical_not(twice))
-        def _():
-            passed_across(*PASSED[LAST])
-
         def rows_sent(k):
             shared_rows = STEP * (2 * MOST + sum(LEFT[lane][(k + 4) % Z] - LEFT[lane][k] for lane in range(2)))
             return 4 * D_EXPERT + 2 * (D_EXPERT - MOST * STEP) + shared_rows + TWICE * (k in (3, 7))
 
-        for n in sorted({rows_sent(k) for k in range(Z)}):
-            @pl.when(at_plane([int(rows_sent(k) == n) for k in range(Z)]) > 0)
+        sent(ring.at[c, y, x, 0:7], r_send.at[0])
+        sent(held.at[0, 0:168, 0:768], r_send.at[1])
+        twice = z == 1
+
+        @pl.when(twice)
+        def _():
+            sent(gate.at[0 : rows_sent(1) // SHARDS, :], ici_send)
+
+        arrived(TWICE, passed_recv.at[LAST])
+
+        @pl.when(jnp.logical_not(twice))
+        def _():
+            passed_across(*PASSED[LAST])
+
+        for n in sorted({rows_sent(k) for k in range(Z) if k != 1}):
+            @pl.when(at_plane([int(k != 1 and rows_sent(k) == n) for k in range(Z)]) > 0)
             def _():
                 sent(gate.at[0 : n // SHARDS, :], ici_send)
-        sent(ring.at[c, y, x, 0:7], r_send.at[0])
-        sent(held.at[0, 0:168, 0:768], r_send.at[1])
 
         def swapped(ref):
             sent(ref, core_sem.at[0])

time: 82 us -> 82 us (level)
  no operation moved by 1% of the time
where the time goes in v9:
time: 82 us; the launch traced here: 81.9 us
  Pallas kernels  80.6 us (98%)
  between operations  1.29 us (2%)
    pallas_call x1, Pallas kernels, local(): pl.pallas_call(kernel, out_shape=outs, in_specs=[hbm] * 6 + [vmem], out_s...  77.2 us
    pallas_call x1, Pallas kernels, local(): pl.pallas_call(store, out_shape=outs, in_specs=[vmem] * 3, out_specs=(hbm...  3.42 us

profile of v9, /device:TPU:121, one launch (start us, length us, event | category | flops | bytes accessed | tf_op | source)
XLA Modules:
  0.0 81.9 jit_solution(8654630366051434503)
XLA Ops:
  1.3 77.2 %mix_and_gather.1 = (bf16[1024,2048]{1,0:T(8,128)(2,1)S(1)}, bf16[1024,2048]{1,0:T(8,128)(2,1)S(1)}, bf16[64,2048]{1,0:T(8,128)(2,1)S(1)}) custom-call(f32[1,256,1024]{2,1,0:T(8,128)} %wg.1, f32[1,256,1024]{2,1,0:T(8,128)} %ag.1, f32[1,256,1024]{2,1,0:T(8,128)} %wu.1, f32[1,256,1024]{2,1,0:T(8,128)} %au.1, f32[1,256]{1,0:T(1,128)} %bitcast.7, ...), custom_call_target="tpu_custom_call" | custom-call | tf_op jit(solution)/shard_map/mix_and_gather/pallas_call | solution.py:425
  78.5 3.4 %store.1 = (bf16[1024,2048]{1,0:T(8,128)(2,1)}, bf16[1024,2048]{1,0:T(8,128)(2,1)}, bf16[64,2048]{1,0:T(8,128)(2,1)}) custom-call(bf16[1024,2048]{1,0:T(8,128)(2,1)S(1)} %get-tuple-element.9.gate, bf16[1024,2048]{1,0:T(8,128)(2,1)S(1)} %get-tuple-element.10.up, bf16[64,2048]{1,0:T(8,128)(2,1)S(1)} %get-tuple-element.11.router), custom_call_target="tpu_custom_call" | custom-call | tf_op jit(solution)/shard_map/store/pallas_call | solution.py:452

commit v10 on v9

--- a/solution.py
+++ b/solution.py
@@ -117,10 +117,10 @@
         return copy(1 - lane, s, *chunks(*OTHER[i]), lanes[lane], ici_send, second_recv.at[i])
 
     def passed(lane, p, shard):
-        return copy(lane, shard, *PASSED[p], lanes[lane], ici_send, passed_recv.at[p])
+        return copy(lane, shard, *PASSED[p], lanes[lane], ici_send, passed_recv.at[max(p - 1, 0)])
 
     def shared(lane, i, shard, to):
-        return copy(lane, shard, i * STEP, STEP, to, ici_send, passed_recv.at[LAST + 2])
+        return copy(lane, shard, i * STEP, STEP, to, ici_send, passed_recv.at[0])
 
     def across(k, shard, lo, n):
         return copy(k, shard, lo, n, MATE, core_sem.at[0], core_sem.at[1])
@@ -275,7 +275,7 @@
                 for p, (lo, n) in enumerate(PASSED):
                     if start <= lo < start + length:
                         if p == LAST:
-                            again = copy(lane, shard, lo, n, (FORE_MATE, BACK_MATE)[lane], ici_send, passed_recv.at[LAST + 1])
+                            again = copy(lane, shard, lo, n, (FORE_MATE, BACK_MATE)[lane], ici_send, passed_recv.at[LAST])
                             more = z == (7, 3)[lane]
 
                             @pl.when(jnp.logical_and(more, c == 0))
@@ -362,12 +362,13 @@
             across(lane, arriving(lane, 2), lo, n).start()
 
     with jax.named_scope("shared"):
-        arrived(MOST * STEP, passed_recv.at[LAST + 2])
-        passed_across(0, MOST * STEP)
+        arrived(sum(PASSED[1]), passed_recv.at[0])
+        passed_across(0, sum(PASSED[1]))
     for p, (lo, n) in enumerate(PASSED[:LAST]):
-        with jax.named_scope(f"passed{p}"):
-            arrived(n, passed_recv.at[p])
-            passed_across(lo, n)
+        if p > 1:
+            with jax.named_scope(f"passed{p}"):
+                arrived(n, passed_recv.at[p - 1])
+                passed_across(lo, n)
 
     with jax.named_scope("finish"):
         def rows_sent(k):
@@ -382,7 +383,7 @@
         def _():
             sent(gate.at[0 : rows_sent(1) // SHARDS, :], ici_send)
 
-        arrived(TWICE, passed_recv.at[LAST])
+        arrived(TWICE, passed_recv.at[LAST - 1])
 
         @pl.when(jnp.logical_not(twice))
         def _():
@@ -399,7 +400,7 @@
 
         @pl.when(twice)
         def _():
-            arrived(TWICE, passed_recv.at[LAST + 1])
+            arrived(TWICE, passed_recv.at[LAST])
             swapped(gate.at[0 : D_EXPERT - 2 * TWICE // SHARDS, :])
 
         @pl.when(jnp.logical_not(twice))
@@ -437,7 +438,7 @@
             pltpu.SemaphoreType.REGULAR((4,)),
             dma((len(GROUPS),)),
             dma((len(OTHER),)),
-            dma((len(PASSED) + 2,)),
+            dma((len(PASSED),)),
             dma,
             dma((2,)),
             dma((2,)),

time: 82 us -> 82 us (level)
  no operation moved by 1% of the time
where the time goes in v10:
time: 82 us; the launch traced here: 81.9 us
  Pallas kernels  80.6 us (98%)
  between operations  1.29 us (2%)
    pallas_call x1, Pallas kernels, local(): pl.pallas_call(kernel, out_shape=outs, in_specs=[hbm] * 6 + [vmem], out_s...  77.2 us
    pallas_call x1, Pallas kernels, local(): pl.pallas_call(store, out_shape=outs, in_specs=[vmem] * 3, out_specs=(hbm...  3.42 us

profile of v10, /device:TPU:121, one launch (start us, length us, event | category | flops | bytes accessed | tf_op | source)
XLA Modules:
  0.0 81.9 jit_solution(13197372411112216736)
XLA Ops:
  1.3 77.2 %mix_and_gather.1 = (bf16[1024,2048]{1,0:T(8,128)(2,1)S(1)}, bf16[1024,2048]{1,0:T(8,128)(2,1)S(1)}, bf16[64,2048]{1,0:T(8,128)(2,1)S(1)}) custom-call(f32[1,256,1024]{2,1,0:T(8,128)} %wg.1, f32[1,256,1024]{2,1,0:T(8,128)} %ag.1, f32[1,256,1024]{2,1,0:T(8,128)} %wu.1, f32[1,256,1024]{2,1,0:T(8,128)} %au.1, f32[1,256]{1,0:T(1,128)} %bitcast.7, ...), custom_call_target="tpu_custom_call" | custom-call | tf_op jit(solution)/shard_map/mix_and_gather/pallas_call | solution.py:426
  78.5 3.4 %store.1 = (bf16[1024,2048]{1,0:T(8,128)(2,1)}, bf16[1024,2048]{1,0:T(8,128)(2,1)}, bf16[64,2048]{1,0:T(8,128)(2,1)}) custom-call(bf16[1024,2048]{1,0:T(8,128)(2,1)S(1)} %get-tuple-element.9.gate, bf16[1024,2048]{1,0:T(8,128)(2,1)S(1)} %get-tuple-element.10.up, bf16[64,2048]{1,0:T(8,128)(2,1)S(1)} %get-tuple-element.11.router), custom_call_target="tpu_custom_call" | custom-call | tf_op jit(solution)/shard_map/store/pallas_call | solution.py:453

commit v11 on v9

--- a/solution.py
+++ b/solution.py
@@ -19,7 +19,7 @@
 STEP, MOST = 64, 4
 PASSED = ((MOST * STEP, 256), (512, 256), (768, 128), (896, 128 - TWICE), (1024 - TWICE, TWICE))
 LAST = len(PASSED) - 1
-LEFT = (0, 0, 0, 0, 0, 0, 4, 0), (3, 0, 0, 0, 2, 1, 0, 0)
+LEFT = (0, 0, 0, 0, 0, 0, 4, 0), (4, 0, 0, 0, 2, 1, 0, 0)
 LATE = 6
 
 

time: 82 us -> 82.1 us (level)
  the two profiles are of different devices: /device:TPU:121 before, /device:TPU:441 now
where the time goes in v11:
time: 82.1 us; the launch traced here: 82 us
  Pallas kernels  80.7 us (98%)
  between operations  1.29 us (2%)
    pallas_call x1, Pallas kernels, local(): pl.pallas_call(kernel, out_shape=outs, in_specs=[hbm] * 6 + [vmem], out_s...  77.3 us
    pallas_call x1, Pallas kernels, local(): pl.pallas_call(store, out_shape=outs, in_specs=[vmem] * 3, out_specs=(hbm...  3.42 us

profile of v11, /device:TPU:441, one launch (start us, length us, event | category | flops | bytes accessed | tf_op | source)
XLA Modules:
  0.0 82.0 jit_solution(12541403041198813729)
XLA Ops:
  1.3 77.3 %mix_and_gather.1 = (bf16[1024,2048]{1,0:T(8,128)(2,1)S(1)}, bf16[1024,2048]{1,0:T(8,128)(2,1)S(1)}, bf16[64,2048]{1,0:T(8,128)(2,1)S(1)}) custom-call(f32[1,256,1024]{2,1,0:T(8,128)} %wg.1, f32[1,256,1024]{2,1,0:T(8,128)} %ag.1, f32[1,256,1024]{2,1,0:T(8,128)} %wu.1, f32[1,256,1024]{2,1,0:T(8,128)} %au.1, f32[1,256]{1,0:T(1,128)} %bitcast.7, ...), custom_call_target="tpu_custom_call" | custom-call | tf_op jit(solution)/shard_map/mix_and_gather/pallas_call | solution.py:425
  78.6 3.4 %store.1 = (bf16[1024,2048]{1,0:T(8,128)(2,1)}, bf16[1024,2048]{1,0:T(8,128)(2,1)}, bf16[64,2048]{1,0:T(8,128)(2,1)}) custom-call(bf16[1024,2048]{1,0:T(8,128)(2,1)S(1)} %get-tuple-element.9.gate, bf16[1024,2048]{1,0:T(8,128)(2,1)S(1)} %get-tuple-element.10.up, bf16[64,2048]{1,0:T(8,128)(2,1)S(1)} %get-tuple-element.11.router), custom_call_target="tpu_custom_call" | custom-call | tf_op jit(solution)/shard_map/store/pallas_call | solution.py:452
